TPU v7x, 512 devices: a 8x2x16 block of a 8x8x16 slice. The times are simulated.
512 devices in a mesh: grp: 2 (over y), ctx: 32 (over z, core), hd: 8 (over x).
Axes of the slice: x: 8, y: 2, z: 16, core: 2. Of those that a mesh axis runs over, the one named last changes fastest.
The devices are a block of a 8x8x16 slice.
Arguments:
- query: bfloat16 [8192, 4096], P(('grp', 'ctx'), 'hd'), parts along dimension 0, may hold values from -6 to 6
- keys: bfloat16 [8192, 1024], P(('grp', 'ctx'), 'hd'), parts along dimension 0, may hold values from -6 to 6
- values: bfloat16 [8192, 1024], P(('grp', 'ctx'), 'hd'), parts along dimension 0, may hold values from -6 to 6
- m_x: bfloat16 [8192, 8192], P(('grp', 'ctx'), 'hd'), parts along dimension 0, may hold values from -6 to 6
- m_z: bfloat16 [8192, 8192], P(('grp', 'ctx'), 'hd'), parts along dimension 0, may hold values from -6 to 6
- m_b: bfloat16 [8192, 1024], P(('grp', 'ctx'), 'hd'), parts along dimension 0, may hold values from -6 to 6
- m_c: bfloat16 [8192, 1024], P(('grp', 'ctx'), 'hd'), parts along dimension 0, may hold values from -0.5 to 0.5
- dt_raw: bfloat16 [8192, 128], P(('grp', 'ctx'), 'hd'), parts along dimension 0, may hold values from -5 to 204
- dt_bias: float32 [128], P('hd'), may hold values from -0.5 to 0.5
- a_log: float32 [128], P('hd'), may hold values from -10 to 0
- d_skip: float32 [128], P('hd'), may hold values from 0.5 to 2
- norm_gain: float32 [8192], P('hd'), may hold values from 0.5 to 1.5
Outputs:
- context: bfloat16 [8192, 4096], P(('grp', 'ctx'), 'hd'), parts along dimension 0
- mixed: bfloat16 [8192, 8192], P(('grp', 'ctx'), 'hd'), parts along dimension 0
There are 2 independent parts, one for each index of `grp`. A program takes and returns all parts, laid end to end along the dimension named above; an argument that names none is the same for every part. Nothing has to cross between parts.
All inputs are finite; a program needn't handle non-finite values.
Results may differ from a plain program's by a relative error of at most 0.009.
Values may be sent and summed in bfloat16 or wider, within the bound.
No kernel may reach another device: no remote copies, remote signals or barrier semaphores. Data moves between devices by JAX's collectives and lax.ppermute only.
A program may use at most 64 MiB of HBM per device.

v0:
```python
import math

import jax
import jax.numpy as jnp
from jax import lax
from jax.sharding import Mesh
from jax.sharding import PartitionSpec as P

HEAD_SIZE = 128
MP = 64
MN = 128
CTX = ("ctx_0", "ctx_1")
GRP_CTX = ("grp", "ctx_0", "ctx_1")


norm_eps = 1e-05
masked_score = -1e30


def in_order(blocks, dim):
    blocks = jnp.moveaxis(blocks, 0, dim)
    shape = blocks.shape
    return blocks.reshape(*shape[:dim], shape[dim] * shape[dim + 1], *shape[dim + 2 :])


def stacked_from(shard, axes, order):
    blocks = shard
    for k in order:
        blocks = lax.all_gather(blocks, axes[k])
    done = order[::-1]
    back = [done.index(k) for k in range(len(axes))]
    blocks = blocks.transpose(*back, *range(len(axes), blocks.ndim))
    return blocks.reshape(-1, *shard.shape)


def gather_axes(shard, axes, order, dim):
    return in_order(stacked_from(shard, axes, order), dim)


def sent_together(arrays, axis, dim, along):
    ends, at = ([], 0)
    for a in arrays[:-1]:
        at += a.shape[along]
        ends.append(at)
    both = jnp.concatenate(arrays, axis=along)
    return tuple(jnp.split(lax.all_gather(both, axis, axis=dim, tiled=True), ends, axis=along))


def token_position(row_index, tok_rows, ctx_count):
    device = row_index // tok_rows
    within = row_index - device * tok_rows
    half_rows = tok_rows // 2
    second = within >= half_rows
    block_index = jnp.where(second, 2 * ctx_count - 1 - device, device)
    return block_index * half_rows + within - jnp.where(second, half_rows, 0)


def pick_block(total_rows, limit):
    selected = 1
    for candidate in range(1, min(total_rows, limit) + 1):
        if total_rows % candidate == 0:
            selected = candidate
    return selected


def folded_to_sequence(whole, ctx_count):
    half_rows = whole.shape[0] // (2 * ctx_count)
    blocks = whole.reshape((ctx_count, 2, half_rows) + whole.shape[1:])
    return jnp.concatenate([blocks[:, 0], blocks[::-1, 1]], axis=0).reshape(whole.shape)


def attend(query, keys, values):
    tok_rows = query.shape[0]
    ctx_count = lax.axis_size(CTX)
    kv_local = keys.shape[1] // HEAD_SIZE
    heads_per_group = query.shape[1] // keys.shape[1]
    query_heads = query.reshape(tok_rows, kv_local, heads_per_group, HEAD_SIZE)
    own_rows = lax.axis_index(CTX) * tok_rows + jnp.arange(tok_rows, dtype=jnp.int32)
    query_pos = token_position(own_rows, tok_rows, ctx_count)
    scaling = 1.0 / math.sqrt(HEAD_SIZE)
    start_max = jnp.full((kv_local, heads_per_group, tok_rows), masked_score, jnp.float32)
    start_sum = jnp.zeros((kv_local, heads_per_group, tok_rows), jnp.float32)
    start_acc = jnp.zeros((kv_local, heads_per_group, tok_rows, HEAD_SIZE), jnp.float32)
    start = jnp.int32(0)
    key_piece = gather_axes(keys, CTX, (0, 1), 0)
    value_piece = gather_axes(values, CTX, (0, 1), 0)
    piece_rows = key_piece.shape[0]
    rows_per_block = pick_block(piece_rows, 1024)

    def one_block(index, running):
        running_max, running_sum, running_acc = running
        offset = index * rows_per_block
        key_block = lax.dynamic_slice_in_dim(key_piece, offset, rows_per_block, 0).reshape(
            rows_per_block, kv_local, HEAD_SIZE
        )
        value_block = lax.dynamic_slice_in_dim(value_piece, offset, rows_per_block, 0).reshape(
            rows_per_block, kv_local, HEAD_SIZE
        )
        key_pos = token_position(
            start + offset + jnp.arange(rows_per_block, dtype=jnp.int32), tok_rows, ctx_count
        )
        visible = key_pos[None, :] <= query_pos[:, None]
        scores = (
            jnp.einsum("qhgd,khd->hgqk", query_heads, key_block, preferred_element_type=jnp.float32)
            * scaling
        )
        scores = jnp.where(visible, scores, masked_score)
        new_max = jnp.maximum(running_max, jnp.max(scores, axis=-1))
        weights = jnp.where(visible, jnp.exp(scores - new_max[..., None]), 0.0)
        factor = jnp.exp(running_max - new_max)
        new_sum = running_sum * factor + jnp.sum(weights, axis=-1)
        update = jnp.einsum(
            "hgqk,khd->hgqd",
            weights.astype(jnp.bfloat16),
            value_block,
            preferred_element_type=jnp.float32,
        )
        return (new_max, new_sum, running_acc * factor[..., None] + update)

    final_max, final_sum, final_acc = lax.fori_loop(
        0, piece_rows // rows_per_block, one_block, (start_max, start_sum, start_acc)
    )
    averaged = final_acc / final_sum[..., None]
    return jnp.transpose(averaged, (2, 0, 1, 3)).reshape(tok_rows, -1).astype(jnp.bfloat16)


def ssd_block(inputs, steps, rates, b_rows, c_rows):
    intersection = jnp.dot(c_rows, b_rows.T, preferred_element_type=jnp.float32)
    inputs = inputs.astype(jnp.float32)
    b_rows = b_rows.astype(jnp.float32)
    sequence_length = inputs.shape[0]
    running = jnp.cumsum(-steps * rates, axis=0)
    lower = jnp.arange(sequence_length)[:, None] >= jnp.arange(sequence_length)[None, :]
    spread = running[:, None, :] - running[None, :, :]
    decay = jnp.exp(jnp.where(lower[:, :, None], spread, -jnp.inf))
    weights = intersection[:, :, None] * decay * steps[None, :, :]
    inner = jnp.einsum("ijh,jhp->ihp", weights, inputs)
    tail_weight = jnp.exp(running[-1][None, :] - running) * steps
    state = jnp.einsum("jh,jhp,jn->hpn", tail_weight, inputs, b_rows)
    return (inner, state, jnp.exp(running[-1]), jnp.exp(running))


def chain_states(earlier, later):
    return (earlier[0] * later[0], earlier[1] * later[0][..., None, None] + later[1])


def ssd_sequence(inputs, steps, rates, b_rows, c_rows):
    sequence_length, head_count, width = inputs.shape
    block_len = math.gcd(sequence_length, 128)
    count = sequence_length // block_len
    c_blocks = c_rows.reshape(count, block_len, -1)
    inner, state, totals, scaled = jax.vmap(ssd_block, in_axes=(0, 0, None, 0, 0))(
        inputs.reshape(count, block_len, head_count, width),
        steps.reshape(count, block_len, head_count),
        rates,
        b_rows.reshape(count, block_len, -1),
        c_blocks,
    )
    running = lax.associative_scan(chain_states, (totals, state))
    entering = jnp.concatenate([jnp.zeros_like(running[1][:1]), running[1][:-1]], axis=0)
    carried = (
        jnp.einsum("cqn,chpn->cqhp", c_blocks.astype(jnp.float32), entering) * scaled[..., None]
    )
    return (inner + carried).reshape(sequence_length, head_count, width)


def gated_norm(gated_rows, norm_scale, group_count):
    row_count = gated_rows.shape[0]
    widened = (
        lax.optimization_barrier(gated_rows).astype(jnp.float32).reshape(row_count, group_count, -1)
    )
    power = jnp.mean(widened * widened, axis=-1, keepdims=True)
    return ((widened * lax.rsqrt(power + norm_eps)).reshape(row_count, -1) * norm_scale).astype(
        jnp.bfloat16
    )


def body(query, keys, values, m_x, m_z, m_b, m_c, dt_raw, dt_bias, a_log, d_skip, norm_gain):
    ctx_count = lax.axis_size(CTX)
    context_fold = attend(query, keys, values)
    groups_here = m_b.shape[1] // MN
    rates = jnp.exp(a_log)
    x_cols, z_cols, context_cols = (
        lax.all_to_all(m_x, CTX, split_axis=1, concat_axis=0, tiled=True),
        lax.all_to_all(m_z, CTX, split_axis=1, concat_axis=0, tiled=True),
        lax.all_to_all(context_fold, CTX, split_axis=1, concat_axis=0, tiled=True),
    )
    dt_whole, b_whole, c_whole = sent_together((dt_raw, m_b, m_c), CTX, 0, 1)
    x_cols = folded_to_sequence(x_cols, ctx_count)
    z_cols = folded_to_sequence(z_cols, ctx_count)
    context_cols = folded_to_sequence(context_cols, ctx_count)
    dt_whole = folded_to_sequence(dt_whole, ctx_count)
    b_whole = folded_to_sequence(b_whole, ctx_count)
    c_whole = folded_to_sequence(c_whole, ctx_count)
    sequence_length = x_cols.shape[0]
    width = x_cols.shape[1]
    sub_width = min(width, MP)
    head_count = width // sub_width
    first_head = lax.axis_index(CTX) * width // MP
    step_mine = jax.nn.softplus(
        lax.dynamic_slice_in_dim(dt_whole, first_head, head_count, 1).astype(jnp.float32)
        + lax.dynamic_slice_in_dim(dt_bias, first_head, head_count, 0)
    )
    rate_mine = lax.dynamic_slice_in_dim(rates, first_head, head_count, 0)
    skip_mine = lax.dynamic_slice_in_dim(d_skip, first_head, head_count, 0)
    x_mine = x_cols.reshape(sequence_length, head_count, sub_width)
    outputs = ssd_sequence(x_mine, step_mine, rate_mine, b_whole, c_whole)
    outputs = outputs + skip_mine[None, :, None] * x_mine.astype(jnp.float32)
    gated = (
        outputs.reshape(sequence_length, width) * jax.nn.silu(z_cols.astype(jnp.float32))
    ).astype(jnp.bfloat16)
    gated_rows, context = (
        lax.all_to_all(gated, CTX, split_axis=0, concat_axis=1, tiled=True),
        lax.all_to_all(context_cols, CTX, split_axis=0, concat_axis=1, tiled=True),
    )
    mixed = gated_norm(gated_rows, norm_gain, groups_here)
    return (context, mixed)


def solution(mesh):
    split = Mesh(
        mesh.devices.reshape(mesh.shape["grp"], 16, 2, mesh.shape["hd"]),
        ("grp", "ctx_0", "ctx_1", "hd"),
    )
    return jax.shard_map(
        body,
        mesh=split,
        in_specs=(
            P(GRP_CTX, "hd"),
            P(GRP_CTX, "hd"),
            P(GRP_CTX, "hd"),
            P(GRP_CTX, "hd"),
            P(GRP_CTX, "hd"),
            P(GRP_CTX, "hd"),
            P(GRP_CTX, "hd"),
            P(GRP_CTX, "hd"),
            P("hd"),
            P("hd"),
            P("hd"),
            P("hd"),
        ),
        out_specs=(P(GRP_CTX, "hd"), P(GRP_CTX, "hd")),
        check_vma=False,
    )
```

profile of v0, /device:TPU:65, one launch (start us, length us, event | category | flops | bytes accessed | tf_op | source)
XLA Modules:
  0.0 289.9 jit_solution(6494011130567231543)
XLA Ops:
  7.3 67.5 %all-gather = bf16[2048,128]{1,0:T(8,128)(2,1)} all-gather(bf16[128,128]{1,0:T(8,128)(2,1)} %param.15), channel_id=2, replica_groups=mesh['grp'=2,'ctx_0'=16,'ctx_1'=2,'hd'=8] {'ctx_0'}, dimensions={0}, use_global_device_ids=true | all-gather | bytes 557056 | tf_op jit(solution)/shard_map/all_gather | solution.py:29
  75.0 25.6 %all-gather.2 = bf16[2048,128]{1,0:T(8,128)(2,1)} all-gather(bf16[128,128]{1,0:T(8,128)(2,1)} %param.16), channel_id=4, replica_groups=mesh['grp'=2,'ctx_0'=16,'ctx_1'=2,'hd'=8] {'ctx_0'}, dimensions={0}, use_global_device_ids=true | all-gather | bytes 557056 | tf_op jit(solution)/shard_map/all_gather | solution.py:29
  101.5 18.2 %all-to-all-start.2 = ((bf16[128,32,32]{0,2,1:T(8,128)(2,1)}), bf16[128,32,32]{0,2,1:T(8,128)(2,1)S(1)}, u32[]{:S(2)}, u32[]{:S(2)}) async-start(bf16[128,32,32]{0,2,1:T(8,128)(2,1)} %bitcast.17), calls=%async_computation.2 | async-start | bytes 524288 | tf_op jit(solution)/shard_map/all_to_all | solution.py:184
  124.4 17.4 %all-to-all-done.2 = bf16[128,32,32]{0,2,1:T(8,128)(2,1)S(1)} async-done(((bf16[128,32,32]{0,2,1:T(8,128)(2,1)}), bf16[128,32,32]{0,2,1:T(8,128)(2,1)S(1)}, u32[]{:S(2)}, u32[]{:S(2)}) %all-to-all-start.2) | async-done | bytes 262176 | tf_op jit(solution)/shard_map/all_to_all | solution.py:184
  141.9 5.0 %all-to-all-start.3 = ((bf16[128,32,32]{0,2,1:T(8,128)(2,1)}), bf16[128,32,32]{0,2,1:T(8,128)(2,1)}, u32[]{:S(2)}, u32[]{:S(2)}) async-start(bf16[128,32,32]{0,2,1:T(8,128)(2,1)} %bitcast.54), calls=%async_computation.3 | async-start | bytes 524288 | tf_op jit(solution)/shard_map/all_to_all | solution.py:185
  149.9 1.4 copy.146
  151.3 2.4 copy.148
  153.7 16.5 %while.20 = (s32[]{:T(128)}, f32[1,4,128]{2,1,0:T(4,128)S(1)}, f32[1,4,128]{2,1,0:T(4,128)S(1)}, f32[1,4,128,128]{3,2,1,0:T(8,128)}, bf16[4096,128]{1,0:T(8,128)...) while((s32[]{:T(128)}, f32[1,4,128]{2,1,0:T(4,128)S(1)}, ...), condition=%wide.region_3.4_spmd.clone, body=%wide.region_0.3_spmd.clone.sunk | while | flops 275610752 | bytes 10134783 | solution.py:120
  155.3 1.8 fusion.98
  159.4 1.8 fusion.98
  163.6 1.8 fusion.98
  167.7 1.8 fusion.98
  170.2 1.1 copy.150
  172.0 12.6 %all-to-all-start = ((bf16[128,32,16]{0,2,1:T(8,128)(2,1)}), bf16[128,32,16]{0,2,1:T(8,128)(2,1)S(1)}, u32[]{:S(2)}, u32[]{:S(2)}) async-start(bf16[128,32,16]{0,2,1:T(8,128)(2,1)} %bitcast.11), calls=%async_computation | async-start | bytes 262144 | tf_op jit(solution)/shard_map/all_to_all | solution.py:186
  184.6 1.2 pad_maximum_fusion.2
  186.0 1.3 reshape.332
  189.9 11.9 %all-to-all-done = bf16[128,32,16]{0,2,1:T(8,128)(2,1)S(1)} async-done(((bf16[128,32,16]{0,2,1:T(8,128)(2,1)}), bf16[128,32,16]{0,2,1:T(8,128)(2,1)S(1)}, u32[]{:S(2)}, u32[]{:S(2)}) %all-to-all-start) | async-done | bytes 131104 | tf_op jit(solution)/shard_map/all_to_all | solution.py:186
  203.5 5.5 %all-to-all-start.1 = ((bf16[32,128,16]{1,2,0:T(8,128)(2,1)}), bf16[32,128,16]{1,2,0:T(8,128)(2,1)}, u32[]{:S(2)}, u32[]{:S(2)}) async-start(bf16[32,128,16]{1,2,0:T(8,128)(2,1)} %copy.153), calls=%async_computation.1 | async-start | bytes 262144 | tf_op jit(solution)/shard_map/all_to_all | solution.py:214
  209.0 4.6 %all-gather.8.cloned.1.call-done = bf16[4096,272]{1,0:T(8,128)(2,1)} async-done(((bf16[128,272]{1,0:T(8,128)(2,1)}), bf16[4096,272]{1,0:T(8,128)(2,1)}) %all-gather.8.cloned.1.call-update) | async-done | bytes 2228240 | tf_op jit(solution)/shard_map/all_gather | solution.py:46
  213.6 1.2 slice-done
  216.5 1.4 negate_multiply_fusion
  218.0 2.9 copy.166
  220.8 1.8 fusion.77
  222.6 1.3 copy.167
  226.8 2.9 %fusion.71 = (bf16[4096,128]{1,0:T(8,128)(2,1)S(1)}, bf16[4096,128]{1,0:T(8,128)(2,1)S(1)}) fusion(bf16[4096,272]{1,0:T(8,128)(2,1)} %all-gather.8.cloned.1.call-done), kind=kLoop, calls=%fused_computation.137 | loop fusion | bytes 4194304 | tf_op jit(solution)/shard_map/split | solution.py:46
  238.1 5.8 %pad.103 = f32[32,1,32,128]{3,2,0,1:T(8,128)S(1)} pad(f32[16,1,32,128]{3,2,0,1:T(8,128)} %add.239, f32[]{:T(128)} %constant.191.clone.1), padding=1_0_1x0_0_0x0_0_0x0_0_0 | pad | bytes 786436
  243.9 1.1 pad_maximum_fusion
  245.0 3.5 %fusion.41 = f32[32,128,1,32]{1,3,0,2:T(8,128)} fusion(bf16[32,128,128]{2,1,0:T(8,128)(2,1)} %bitcast.209, bf16[32,128,128]{2,1,0:T(8,128)(2,1)S(1)} %bitcast.197, f32[32,128]{1,0:T(8,128)S(1)} %bitcast.228, f32[32,128]{1,0:T(8,128)S(1)} %bitcast.226, pred[128,128]{1,0:T(8,128)(4,1)S(1)} %copy-done.13, bf16[32,128,32]{1,0,2:T(8,128)(2,1)S(1)} %copy-done.1), kind=kOutput, calls=%fused_computation.63 | convolution fusion | flops 169869312 | bytes 2932736 | tf_op jit(solution)/shard_map/vmap(ijh,jhp->ihp)/dot_general | solution.py:137
  248.6 3.2 %fusion.48 = bf16[32,128,32]{1,2,0:T(8,128)(2,1)} fusion(f32[32,128,1,32]{1,3,0,2:T(8,128)} %fusion.41, bf16[32,128,128]{2,1,0:T(8,128)(2,1)S(1)} %bitcast.210, f32[32,128,32]{1,0,2:T(8,128)} %reshape.333, bf16[31,1,32,128]{3,2,0,1:T(8,128)(2,1)S(1)} %slice_add_fusion.5, f32[]{:T(128)} %bitcast.53, f32[32,128]{1,0:T(8,128)S(1)} %copy-done.14, ...), kind=kOutput, calls=%fused_computation.68 | convolution fusion | flops 34996224 | bytes 2891780 | tf_op jit(solution)/shard_map/cqn,chpn->cqhp/dot_general | solution.py:162
  251.8 8.3 %all-to-all-start.4 = ((bf16[32,128,32]{1,2,0:T(8,128)(2,1)}), bf16[32,128,32]{1,2,0:T(8,128)(2,1)S(1)}, u32[]{:S(2)}, u32[]{:S(2)}) async-start(bf16[32,128,32]{1,2,0:T(8,128)(2,1)} %fusion.48), calls=%async_computation.4 | async-start | bytes 524288 | tf_op jit(solution)/shard_map/all_to_all | solution.py:213
  260.1 1.7 copy.176
  261.8 20.4 %all-to-all-done.4 = bf16[32,128,32]{1,2,0:T(8,128)(2,1)S(1)} async-done(((bf16[32,128,32]{1,2,0:T(8,128)(2,1)}), bf16[32,128,32]{1,2,0:T(8,128)(2,1)S(1)}, u32[]{:S(2)}, u32[]{:S(2)}) %all-to-all-start.4) | async-done | bytes 262176 | tf_op jit(solution)/shard_map/all_to_all | solution.py:213
  (195 shorter events, 37.0 us)
Async XLA Ops:
  7.2 93.4 %copy-start.3 = (bf16[128,1024]{1,0:T(8,128)(2,1)S(1)}, bf16[128,1024]{1,0:T(8,128)(2,1)}, u32[]{:S(2)}) copy-start(bf16[128,1024]{1,0:T(8,128)(2,1)} %param.17) | copy-start | bytes 786436
  7.2 112.6 %copy-start.16 = (bf16[128,16]{0,1:T(8,128)(2,1)S(1)}, bf16[128,16]{0,1:T(8,128)(2,1)}, u32[]{:S(2)}) copy-start(bf16[128,16]{0,1:T(8,128)(2,1)} %param.21) | copy-start | bytes 12292
  7.2 112.8 %copy-start.11 = (bf16[128,128]{1,0:T(8,128)(2,1)S(1)}, bf16[128,128]{1,0:T(8,128)(2,1)}, u32[]{:S(2)}) copy-start(bf16[128,128]{1,0:T(8,128)(2,1)} %param.20) | copy-start | bytes 98308
  7.2 112.7 %copy-start.12 = (bf16[128,128]{1,0:T(8,128)(2,1)S(1)}, bf16[128,128]{1,0:T(8,128)(2,1)}, u32[]{:S(2)}) copy-start(bf16[128,128]{1,0:T(8,128)(2,1)} %param.19) | copy-start | bytes 98308
  7.2 113.6 %copy-start.7 = (bf16[128,512]{1,0:T(8,128)(2,1)S(1)}, bf16[128,512]{1,0:T(8,128)(2,1)}, u32[]{:S(2)}) copy-start(bf16[128,512]{1,0:T(8,128)(2,1)} %param.14) | copy-start | bytes 393220
  7.2 113.9 %copy-start.17 = (f32[16]{0:T(128)S(1)}, f32[16]{0:T(128)}, u32[]{:S(2)}) copy-start(f32[16]{0:T(128)} %param.23) | copy-start | bytes 196
  7.2 114.5 %copy-start.18 = (f32[16]{0:T(128)S(1)}, f32[16]{0:T(128)}, u32[]{:S(2)}) copy-start(f32[16]{0:T(128)} %param.22) | copy-start | bytes 196
  7.2 115.2 %copy-start.4 = (bf16[128,1024]{1,0:T(8,128)(2,1)S(1)}, bf16[128,1024]{1,0:T(8,128)(2,1)}, u32[]{:S(2)}) copy-start(bf16[128,1024]{1,0:T(8,128)(2,1)} %param.18) | copy-start | bytes 786436
  7.3 142.6 %all-gather.10.cloned.1.call-start = ((), (), s32[]{:S(2)}) async-start(), calls=%async_computation.6 | async-start | bytes 1572864 | tf_op jit(solution)/shard_map/all_gather | solution.py:29
  74.8 48.4 %copy-start.19 = (f32[16]{0:T(128)S(1)}, f32[16]{0:T(128)}, u32[]{:S(2)}) copy-start(f32[16]{0:T(128)} %param.24) | copy-start | bytes 196
  74.9 76.4 %all-gather.12.cloned.1.call-start = ((), (), s32[]{:S(2)}) async-start(), calls=%async_computation.7 | async-start | bytes 1572864 | tf_op jit(solution)/shard_map/all_gather | solution.py:29
  101.5 40.4 %all-to-all-start.2 = ((bf16[128,32,32]{0,2,1:T(8,128)(2,1)}), bf16[128,32,32]{0,2,1:T(8,128)(2,1)S(1)}, u32[]{:S(2)}, u32[]{:S(2)}) async-start(bf16[128,32,32]{0,2,1:T(8,128)(2,1)} %bitcast.17), calls=%async_computation.2 | async-start | bytes 524288 | tf_op jit(solution)/shard_map/all_to_all | solution.py:184
  119.7 93.9 %all-gather.8.cloned.1.call-start = ((), (), s32[]{:S(2)}) async-start(), calls=%async_computation.5 | async-start | bytes 3244032 | tf_op jit(solution)/shard_map/all_gather | solution.py:46
  141.9 30.1 %all-to-all-start.3 = ((bf16[128,32,32]{0,2,1:T(8,128)(2,1)}), bf16[128,32,32]{0,2,1:T(8,128)(2,1)}, u32[]{:S(2)}, u32[]{:S(2)}) async-start(bf16[128,32,32]{0,2,1:T(8,128)(2,1)} %bitcast.54), calls=%async_computation.3 | async-start | bytes 524288 | tf_op jit(solution)/shard_map/all_to_all | solution.py:185
  154.4 1.0 copy-start.5
  157.1 0.7 copy-start.6
  158.5 1.0 copy-start.5
  162.6 1.0 copy-start.5
  166.8 1.0 copy-start.5
  172.0 29.9 %all-to-all-start = ((bf16[128,32,16]{0,2,1:T(8,128)(2,1)}), bf16[128,32,16]{0,2,1:T(8,128)(2,1)S(1)}, u32[]{:S(2)}, u32[]{:S(2)}) async-start(bf16[128,32,16]{0,2,1:T(8,128)(2,1)} %bitcast.11), calls=%async_computation | async-start | bytes 262144 | tf_op jit(solution)/shard_map/all_to_all | solution.py:186
  186.0 44.7 %copy-start = (bf16[32,128,32]{1,0,2:T(8,128)(2,1)}, bf16[32,128,32]{1,0,2:T(8,128)(2,1)S(1)}, u32[]{:S(2)}) copy-start(bf16[32,128,32]{1,0,2:T(8,128)(2,1)S(1)} %reshape.325) | copy-start | bytes 786436
  203.5 48.3 %all-to-all-start.1 = ((bf16[32,128,16]{1,2,0:T(8,128)(2,1)}), bf16[32,128,16]{1,2,0:T(8,128)(2,1)}, u32[]{:S(2)}, u32[]{:S(2)}) async-start(bf16[32,128,16]{1,2,0:T(8,128)(2,1)} %copy.153), calls=%async_computation.1 | async-start | bytes 262144 | tf_op jit(solution)/shard_map/all_to_all | solution.py:214
  213.6 1.2 slice-start
  218.0 12.2 %copy-start.9 = (f32[4096,1]{0,1:T(1,128)}, f32[4096,1]{0,1:T(1,128)S(1)}, u32[]{:S(2)}) copy-start(f32[4096,1]{0,1:T(1,128)S(1)} %get-tuple-element.305) | copy-start | bytes 49156
  234.9 3.0 %copy-start.8 = (f32[1,1,32,128]{3,2,0,1:T(8,128)S(1)}, f32[1,1,32,128]{3,2,0,1:T(8,128)}, u32[]{:S(2)}) copy-start(f32[1,1,32,128]{3,2,0,1:T(8,128)} %slice_bitcast_fusion.4) | copy-start | bytes 49156
  237.9 7.1 %copy-start.1 = (bf16[32,128,32]{1,0,2:T(8,128)(2,1)S(1)}, bf16[32,128,32]{1,0,2:T(8,128)(2,1)}, u32[]{:S(2)}) copy-start(bf16[32,128,32]{1,0,2:T(8,128)(2,1)} %copy-done) | copy-start | bytes 786436
  237.9 7.1 %copy-start.10 = (f32[4096,1]{0,1:T(1,128)S(1)}, f32[4096,1]{0,1:T(1,128)}, u32[]{:S(2)}) copy-start(f32[4096,1]{0,1:T(1,128)} %copy-done.9) | copy-start | bytes 49156
  237.9 7.1 %copy-start.13 = (pred[128,128]{1,0:T(8,128)(4,1)S(1)}, pred[128,128]{1,0:T(8,128)(4,1)}, u32[]{:S(2)}) copy-start(pred[128,128]{1,0:T(8,128)(4,1)} %iota_compare_fusion) | copy-start | bytes 49156
  245.0 3.6 %copy-start.2 = (bf16[64,64,128]{2,1,0:T(8,128)(2,1)S(1)}, bf16[64,64,128]{2,1,0:T(8,128)(2,1)}, u32[]{:S(2)}) copy-start(bf16[64,64,128]{2,1,0:T(8,128)(2,1)} %pad_maximum_fusion) | copy-start | bytes 3145732
  245.0 3.6 %copy-start.14 = (f32[32,128]{1,0:T(8,128)S(1)}, f32[32,128]{1,0:T(8,128)}, u32[]{:S(2)}) copy-start(f32[32,128]{1,0:T(8,128)} %get-tuple-element.326) | copy-start | bytes 49156
  248.6 33.9 %copy-start.15 = (f32[1024]{0:T(1024)S(1)}, f32[1024]{0:T(1024)}, u32[]{:S(2)}) copy-start(f32[1024]{0:T(1024)} %param.25) | copy-start | bytes 12292
  251.8 30.4 %all-to-all-start.4 = ((bf16[32,128,32]{1,2,0:T(8,128)(2,1)}), bf16[32,128,32]{1,2,0:T(8,128)(2,1)S(1)}, u32[]{:S(2)}, u32[]{:S(2)}) async-start(bf16[32,128,32]{1,2,0:T(8,128)(2,1)} %fusion.48), calls=%async_computation.4 | async-start | bytes 524288 | tf_op jit(solution)/shard_map/all_to_all | solution.py:213
  (3 other events, 2.1 us)
Sparse Core Ops, SparseCore 0:
  75.0 23.9 all-gather.9
  101.1 30.5 all-gather.11
  133.9 79.7 all-gather.7
where the time goes:
time: 292 us; the launch traced here: 290 us
  blocking collectives  93.1 us (32%)
  waiting for transfers between devices  54.5 us (19%)
  starting transfers between devices  49.8 us (17%)
  local copies, waits for them, and re-layouts  44.6 us (15%)
  other arithmetic  17.3 us (6%)
  matrix products  15.8 us (5%)
  between operations  14.5 us (5%)
    all_gather x2, blocking collectives, stacked_from(): blocks = lax.all_gather(blocks, axes[k])  93.1 us
    all_to_all x1, waiting for transfers between devices, body(): lax.all_to_all(gated, CTX, split_axis=0, concat_axis=1, tiled=True)  20.4 us
    all_to_all x1, starting transfers between devices, body(): lax.all_to_all(m_x, CTX, split_axis=1, concat_axis=0, tiled=True)  18.2 us
    all_to_all x1, waiting for transfers between devices, body(): lax.all_to_all(m_x, CTX, split_axis=1, concat_axis=0, tiled=True)  17.4 us
    all_to_all x1, starting transfers between devices, body(): lax.all_to_all(context_fold, CTX, split_axis=1, concat_axis=0, tiled=True)  12.6 us
    unnamed x50, local copies, waits for them, and re-layouts  12.3 us
    all_to_all x1, waiting for transfers between devices, body(): lax.all_to_all(context_fold, CTX, split_axis=1, concat_axis=0, tiled=True)  11.9 us
    all_to_all x1, starting transfers between devices, body(): lax.all_to_all(gated, CTX, split_axis=0, concat_axis=1, tiled=True)  8.33 us
  transfers between devices with their start and end apart: 8, of which 4 were waited for; matrix products, arithmetic and copies ran while one was open for 24% of the time, Pallas kernels for 0%

commit v1 on v0

v1 whole, which is shorter than its diff:
```python
import functools
import math

import jax
import jax.numpy as jnp
from jax import lax
from jax.experimental import pallas as pl
from jax.experimental.pallas import tpu as pltpu
from jax.sharding import PartitionSpec as P

HEAD_SIZE = 128
MP = 64
MN = 128
HALF = 64
TOK = 128
CTX = "ctx"
GRP_CTX = ("grp", "ctx")

norm_eps = 1e-05
F32 = jnp.float32
BF16 = jnp.bfloat16
NT = (((1,), (1,)), ((), ()))


def vmem_spec():
    return pl.BlockSpec(memory_space=pltpu.VMEM)


def smem_spec():
    return pl.BlockSpec(memory_space=pltpu.SMEM)


def any_spec():
    return pl.BlockSpec(memory_space=pl.ANY)


def cost(flops, moved):
    return pl.CostEstimate(flops=flops, bytes_accessed=moved, transcendentals=0)


def pack_kernel(k_ref, v_ref, b_ref, c_ref, dt_ref, out_ref):
    out_ref[0:128, :] = k_ref[...]
    out_ref[128:256, :] = v_ref[...]
    out_ref[256:384, :] = b_ref[...]
    out_ref[384:512, :] = c_ref[...]
    out_ref[512:, :] = dt_ref[...].astype(F32).T.astype(BF16)


def pack(keys, values, m_b, m_c, dt_raw):
    rows = 4 * TOK + dt_raw.shape[1]
    return pl.pallas_call(
        pack_kernel,
        out_shape=jax.ShapeDtypeStruct((rows, TOK), BF16),
        in_specs=[vmem_spec()] * 5,
        out_specs=vmem_spec(),
        cost_estimate=cost(10**6, 2 * rows * TOK * 2),
        name="pack",
    )(keys, values, m_b, m_c, dt_raw)


def turn_kernel(count, x_ref, z_ref, out_ref):
    width = x_ref.shape[1] // count
    per_tile = 128 // width
    for tile in range(x_ref.shape[1] // 128):
        columns = slice(tile * 128, tile * 128 + 128)
        for which, ref in enumerate((x_ref, z_ref)):
            turned = ref[:, columns].astype(F32).T.astype(BF16)
            for piece in range(per_tile):
                out_ref[tile * per_tile + piece, which * width : which * width + width, :] = turned[
                    piece * width : piece * width + width, :
                ]


def turn(m_x, m_z, count):
    width = m_x.shape[1] // count
    return pl.pallas_call(
        functools.partial(turn_kernel, count),
        out_shape=jax.ShapeDtypeStruct((count, 2 * width, TOK), BF16),
        in_specs=[vmem_spec()] * 2,
        out_specs=vmem_spec(),
        cost_estimate=cost(10**6, 4 * m_x.size * 2),
        name="turn",
    )(m_x, m_z)


def softplus(v):
    return jnp.maximum(v, 0.0) + jnp.log1p(jnp.exp(-jnp.abs(v)))


def ssd_kernel(count, g_ref, xz_ref, bias_ref, alog_ref, skip_ref, out_ref, bc, run_s, dt_s, end_s, tail_s, sem):
    copy = pltpu.make_async_copy(g_ref.at[:, 2 * TOK :, :], bc, sem)
    copy.start()
    copy.wait()
    width = xz_ref.shape[1] // 2
    me = lax.axis_index(CTX)
    head = (me * width) // MP
    bias, rate, skip = bias_ref[head], jnp.exp(jnp.full((1, 1), alog_ref[head], F32)), skip_ref[head]
    heads = bc.shape[1] - 2 * TOK
    lane = lax.broadcasted_iota(jnp.int32, (1, TOK), 1)
    low = lane < HALF
    mine = lax.broadcasted_iota(jnp.int32, (heads, TOK), 0) == head
    half_count = count // 2

    def dt_row(source):
        rows = bc[source, 2 * TOK :, :].astype(F32)
        return jnp.sum(jnp.where(mine, rows, 0.0), axis=0, keepdims=True)

    for m in range(half_count):
        first, second = dt_row(2 * m), dt_row(2 * m + 1)
        turned = pltpu.roll(second, HALF, 1)
        dt_s[m : m + 1, :] = jnp.where(low, first, turned)
        dt_s[count - 1 - m : count - m, :] = jnp.where(low, turned, first)
    dt = softplus(dt_s[...] + bias)
    dt_s[...] = dt
    run = -dt * rate
    lanes = lax.broadcasted_iota(jnp.int32, (count, TOK), 1)
    shift = 1
    while shift < TOK:
        run = run + jnp.where(lanes >= shift, pltpu.roll(run, shift, 1), 0.0)
        shift *= 2
    run_s[...] = run
    last = jnp.broadcast_to(run[:, TOK - 1 :], (count, TOK))
    end_s[...] = jnp.exp(last)
    tail_s[...] = jnp.exp(last - run) * dt
    row_id = lax.broadcasted_iota(jnp.int32, (TOK, TOK), 0)
    col_id = lax.broadcasted_iota(jnp.int32, (TOK, TOK), 1)
    seen = row_id <= col_id

    def chunk(k, state):
        early = k < half_count
        m = jnp.where(early, k, count - 1 - k)
        base = jnp.where(early, 0, HALF)
        one = jnp.where(early, 2 * m, 2 * m + 1)
        two = jnp.where(early, 2 * m + 1, 2 * m)

        def rows_of(offset):
            start = pl.multiple_of(base + offset, HALF)
            return jnp.concatenate([bc[one, pl.ds(start, HALF), :], bc[two, pl.ds(start, HALF), :]], axis=0)

        b_rows, c_rows = rows_of(0), rows_of(TOK)
        xz_even, xz_odd = xz_ref[2 * m].astype(F32), pltpu.roll(xz_ref[2 * m + 1].astype(F32), HALF, 1)
        xz = jnp.where(low == early, xz_even, xz_odd)
        x, z = xz[:width], xz[width:]
        run_row = jnp.broadcast_to(run_s[pl.ds(k, 1), :], (TOK, TOK))
        decay = jnp.exp(jnp.where(seen, run_row - run_row.T, -jnp.inf))
        cross = lax.dot_general(b_rows, c_rows, NT, preferred_element_type=F32)
        weights = (cross * decay).astype(BF16)
        x_dt = (x * dt_s[pl.ds(k, 1), :]).astype(BF16)
        inner = jnp.dot(x_dt, weights, preferred_element_type=F32)
        x_tail = (x * tail_s[pl.ds(k, 1), :]).astype(BF16)
        added = jnp.dot(x_tail, b_rows, preferred_element_type=F32)
        carried = lax.dot_general(state.astype(BF16), c_rows, NT, preferred_element_type=F32)
        y = inner + carried * jnp.exp(run_s[pl.ds(k, 1), :]) + skip * x
        gated = y * (z / (1.0 + jnp.exp(-z)))
        out_ref[k] = gated.astype(BF16)
        return state * end_s[pl.ds(k, 1), :] + added

    def chunks(step, state):
        for u in range(4):
            state = chunk(step * 4 + u, state)
        return state

    lax.fori_loop(0, count // 4, chunks, jnp.zeros((width, MN), F32))


def ssd(gathered, xz, dt_bias, a_log, d_skip):
    count, rows, _ = gathered.shape
    width = xz.shape[1] // 2
    return pl.pallas_call(
        functools.partial(ssd_kernel, count),
        out_shape=jax.ShapeDtypeStruct((count, width, TOK), BF16),
        in_specs=[any_spec(), vmem_spec(), smem_spec(), smem_spec(), smem_spec()],
        out_specs=vmem_spec(),
        scratch_shapes=[
            pltpu.VMEM((count, rows - 2 * TOK, TOK), BF16),
            pltpu.VMEM((count, TOK), F32),
            pltpu.VMEM((count, TOK), F32),
            pltpu.VMEM((count, TOK), F32),
            pltpu.VMEM((count, TOK), F32),
            pltpu.SemaphoreType.DMA,
        ],
        cost_estimate=cost(10**9, count * rows * TOK),
        name="ssd",
    )(gathered, xz, dt_bias, a_log, d_skip)


def attend_kernel(count, q0_ref, q1_ref, g_ref, out_ref, kv, q_s, m_s, l_s, acc_s, sem):
    copy = pltpu.make_async_copy(g_ref.at[:, : 2 * TOK, :], kv, sem)
    copy.start()
    heads = q0_ref.shape[1] // HEAD_SIZE
    for h in range(heads):
        columns = slice(h * HEAD_SIZE, (h + 1) * HEAD_SIZE)
        q_s[h * TOK : h * TOK + HALF, :] = q0_ref[:, columns]
        q_s[h * TOK + HALF : (h + 1) * TOK, :] = q1_ref[:, columns]
    m_s[...] = jnp.full(m_s.shape, -1e30, F32)
    l_s[...] = jnp.zeros(l_s.shape, F32)
    acc_s[...] = jnp.zeros(acc_s.shape, F32)
    me = lax.axis_index(CTX)
    scale = math.log2(math.e) / math.sqrt(HEAD_SIZE)
    copy.wait()
    blocks = 8
    rows = heads * TOK
    keys_here = blocks * HALF

    def step(index, masked):
        def piece(offset):
            parts = []
            for p in range(blocks):
                c = index * blocks + p
                early = c < count
                source = jnp.where(early, c, 2 * count - 1 - c)
                start = pl.multiple_of(jnp.where(early, 0, HALF) + offset, HALF)
                parts.append(kv[source, pl.ds(start, HALF), :])
            return jnp.concatenate(parts, axis=0)

        k_rows, v_rows = piece(0), piece(TOK)
        scores = lax.dot_general(q_s[...], k_rows, NT, preferred_element_type=F32)
        if masked:
            key_pos = index * keys_here + lax.broadcasted_iota(jnp.int32, (rows, keys_here), 1)
            row = lax.broadcasted_iota(jnp.int32, (rows, keys_here), 0)
            query_pos = me * TOK + jnp.bitwise_and(row, TOK - 1)
            scores = jnp.where(key_pos <= query_pos, scores, -1e30)
        old = m_s[...]
        new = jnp.maximum(old, jnp.max(scores, axis=1, keepdims=True))
        expons = jnp.exp2((scores - new) * scale)
        if masked:
            expons = jnp.where(key_pos <= query_pos, expons, 0.0)
        factor = jnp.exp2((old - new) * scale)
        m_s[...] = new
        l_s[...] = l_s[...] * factor + jnp.sum(expons, axis=1, keepdims=True)
        acc_s[...] = acc_s[...] * factor + jnp.dot(expons.astype(BF16), v_rows, preferred_element_type=F32)

    full = (me * TOK) // keys_here
    lax.fori_loop(0, full, lambda i, _: step(i, False), None)
    step(full, True)
    result = acc_s[...] / l_s[...]
    for h in range(heads):
        out_ref[:, h * HEAD_SIZE : (h + 1) * HEAD_SIZE] = result[h * TOK : (h + 1) * TOK, :].astype(BF16)


def attend(q0, q1, gathered):
    count, rows, _ = gathered.shape
    heads = q0.shape[1] // HEAD_SIZE
    return pl.pallas_call(
        functools.partial(attend_kernel, count),
        out_shape=jax.ShapeDtypeStruct((TOK, q0.shape[1]), BF16),
        in_specs=[vmem_spec(), vmem_spec(), any_spec()],
        out_specs=vmem_spec(),
        scratch_shapes=[
            pltpu.VMEM((count, 2 * TOK, TOK), BF16),
            pltpu.VMEM((heads * TOK, HEAD_SIZE), BF16),
            pltpu.VMEM((heads * TOK, 1), F32),
            pltpu.VMEM((heads * TOK, 1), F32),
            pltpu.VMEM((heads * TOK, HEAD_SIZE), F32),
            pltpu.SemaphoreType.DMA,
        ],
        cost_estimate=cost(4 * heads * TOK * count * TOK * HEAD_SIZE, count * rows * TOK),
        name="attend",
    )(q0, q1, gathered)


def norm_kernel(g_ref, gain_ref, out_ref):
    count, width, _ = g_ref.shape
    channels = count * width
    gated = g_ref[...].astype(F32).reshape(channels, TOK)
    power = jnp.sum(gated * gated, axis=0, keepdims=True) * (1.0 / channels)
    scaled = gated * lax.rsqrt(power + norm_eps)
    for tile in range(channels // 128):
        columns = slice(tile * 128, tile * 128 + 128)
        out_ref[:, columns] = (scaled[columns, :].T * gain_ref[:, columns]).astype(BF16)


def gated_norm(gated, gain):
    count, width, _ = gated.shape
    return pl.pallas_call(
        norm_kernel,
        out_shape=jax.ShapeDtypeStruct((TOK, count * width), BF16),
        in_specs=[vmem_spec()] * 2,
        out_specs=vmem_spec(),
        cost_estimate=cost(10**6, 4 * gated.size),
        name="norm",
    )(gated, gain.reshape(1, -1))


def body(query, keys, values, m_x, m_z, m_b, m_c, dt_raw, dt_bias, a_log, d_skip, norm_gain):
    count = lax.axis_size(CTX)
    me = lax.axis_index(CTX)
    gathered = lax.all_gather(pack(keys, values, m_b, m_c, dt_raw), CTX)
    xz = lax.all_to_all(turn(m_x, m_z, count), CTX, split_axis=0, concat_axis=0, tiled=True)

    parity = lax.rem(me, 2)
    block = [lambda d: d if d % 2 == 0 else 2 * count - 1 - d, lambda d: 2 * count - 1 - d if d % 2 == 0 else d]
    moved = []
    for slot in range(2):
        start = (parity if slot == 0 else 1 - parity) * HALF
        piece = lax.dynamic_slice_in_dim(query, start, HALF, 0)
        moved.append(lax.ppermute(piece, CTX, [(d, block[slot](d) // 2) for d in range(count)]))
    gated = ssd(gathered, xz, dt_bias, a_log, d_skip)
    returned = lax.all_to_all(gated, CTX, split_axis=0, concat_axis=0, tiled=True)
    context = attend(moved[0], moved[1], gathered)
    mixed = gated_norm(returned, norm_gain)
    return (context, mixed)


def solution(mesh):
    rows, heads = P(GRP_CTX, "hd"), P("hd")
    return jax.shard_map(
        body,
        mesh=mesh,
        in_specs=(rows,) * 8 + (heads,) * 4,
        out_specs=(rows, rows),
        check_vma=False,
    )
```

time: 292 us -> 186 us (0.64)
  local copies, waits for them, and re-layouts: 44.6 us -> 2.75 us
  starting transfers between devices: 49.8 us -> 22.4 us
  Pallas kernels: 0 us -> 21 us
  other arithmetic: 17.3 us -> 0 us
  matrix products: 15.8 us -> 0 us
  waiting for transfers between devices: 54.5 us -> 39.3 us
  blocking collectives: 93.1 us -> 83.4 us
    all_gather x2 -> x0, blocking collectives: 93.1 us -> none  [stacked_from(): blocks = lax.all_gather(blocks, axes[k])]
    all_to_all x0 -> x1, blocking collectives: none -> 83.4 us  [body(): lax.all_to_all(turn(m_x, m_z, count), CTX, split_axis=0, concat_axis=0, t...]
    all_to_all x5 -> x1, waiting for transfers between devices: 49.7 us -> 0.68 us  [body(): lax.all_to_all(gated, CTX, split_axis=0, concat_axis=0, tiled=True)]
    all_to_all x5 -> x1, starting transfers between devices: 49.7 us -> 8.15 us  [body(): lax.all_to_all(gated, CTX, split_axis=0, concat_axis=0, tiled=True)]
    all_gather x3 -> x1, waiting for transfers between devices: 4.61 us -> 36.9 us  [body(): gathered = lax.all_gather(pack(keys, values, m_b, m_c, dt_raw), CTX)]
    pallas_call x0 -> x5, Pallas kernels: none -> 21 us  [the longest x1 10.6 us: ssd(): pl.pallas_call(functools.partial(ssd_kernel, count), out_shape=jax.ShapeD...]
    dot_general x11 -> x0, matrix products: 15.8 us -> none  [the longest x4 7.01 us: one_block(): jnp.einsum('hgqk,khd->hgqd', weights.astype(jnp.bfloat16), value_block, p...]
    ppermute x0 -> x2, starting transfers between devices: none -> 14.2 us  [body(): lax.ppermute(piece, CTX, [(d, block[slot](d) // 2) for d in range(count)])]
  transfers between devices with their start and end apart: 8 -> 4, of which waited for: 4 -> 3; matrix products, arithmetic and copies ran while one was open for 24% -> 0% of each run, Pallas kernels for 0% -> 4%
where the time goes in v1:
time: 186 us; the launch traced here: 183 us
  blocking collectives  83.4 us (45%)
  waiting for transfers between devices  39.3 us (21%)
  starting transfers between devices  22.4 us (12%)
  Pallas kernels  21 us (11%)
  between operations  14.1 us (8%)
  local copies, waits for them, and re-layouts  2.75 us (1%)
    all_to_all x1, blocking collectives, body(): lax.all_to_all(turn(m_x, m_z, count), CTX, split_axis=0, concat_axis=0, t...  83.4 us
    all_gather x1, waiting for transfers between devices, body(): gathered = lax.all_gather(pack(keys, values, m_b, m_c, dt_raw), CTX)  36.9 us
    ppermute x2, starting transfers between devices, body(): lax.ppermute(piece, CTX, [(d, block[slot](d) // 2) for d in range(count)])  14.2 us
    pallas_call x1, Pallas kernels, ssd(): pl.pallas_call(functools.partial(ssd_kernel, count), out_shape=jax.ShapeD...  10.6 us
    all_to_all x1, starting transfers between devices, body(): lax.all_to_all(gated, CTX, split_axis=0, concat_axis=0, tiled=True)  8.15 us
    pallas_call x1, Pallas kernels, attend(): pl.pallas_call(functools.partial(attend_kernel, count), out_shape=jax.Sha...  4.86 us
  transfers between devices with their start and end apart: 4, of which 3 were waited for; matrix products, arithmetic and copies ran while one was open for 0% of the time, Pallas kernels for 4%

profile of v1, /device:TPU:65, one launch (start us, length us, event | category | flops | bytes accessed | tf_op | source)
XLA Modules:
  0.0 183.0 jit_solution(227849069824032469)
XLA Ops:
  7.2 0.0 copy-start.1
  7.2 0.1 all-gather.3.cloned.1.call-start
  7.3 1.4 copy.14.dt_ref
  8.7 1.6 pack.1
  10.2 0.1 all-gather.3.cloned.1.call-update
  10.3 2.0 %turn.1 = bf16[32,64,128]{2,1,0:T(8,128)(2,1)} custom-call(bf16[128,1024]{1,0:T(8,128)(2,1)} %x_ref.1, bf16[128,1024]{1,0:T(8,128)(2,1)} %z_ref.1), custom_call_target="tpu_custom_call" | custom-call | flops 1000000 | bytes 1048576 | tf_op jit(solution)/shard_map/turn/pallas_call | solution.py:76
  12.3 83.4 %all_to_all.10.xz_ref = bf16[32,64,128]{2,1,0:T(8,128)(2,1)} all-to-all(bf16[32,64,128]{2,1,0:T(8,128)(2,1)} %turn.1), channel_id=1, replica_groups=mesh['grp'=2,'ctx'=32,'hd'=8] {'ctx'}, dimensions={0} | all-to-all | bytes 1048576 | tf_op jit(solution)/shard_map/all_to_all | solution.py:289
  95.7 36.9 %all-gather.3.cloned.1.call-done = bf16[16896,128]{1,0:T(8,128)(2,1)} async-done(((bf16[528,128]{1,0:T(8,128)(2,1)}), bf16[16896,128]{1,0:T(8,128)(2,1)}) %all-gather.3.cloned.1.call-update) | async-done | bytes 4325392 | tf_op jit(solution)/shard_map/all_gather | solution.py:288
  132.6 10.6 %ssd.1 = bf16[32,32,128]{2,1,0:T(8,128)(2,1)} custom-call(bf16[32,528,128]{2,1,0:T(8,128)(2,1)} %bitcast.2, bf16[32,64,128]{2,1,0:T(8,128)(2,1)} %all_to_all.10.xz_ref, f32[16]{0:T(128)} %bias_ref.1, f32[16]{0:T(128)} %alog_ref.1, f32[16]{0:T(128)} %skip_ref.1), custom_call_target="tpu_custom_call" | custom-call | flops 1000000000 | bytes 2162688 | tf_op jit(solution)/shard_map/ssd/pallas_call | solution.py:169
  143.2 8.1 %all-to-all-start.1 = ((bf16[32,32,128]{2,1,0:T(8,128)(2,1)}), bf16[32,32,128]{2,1,0:T(8,128)(2,1)S(1)}, u32[]{:S(2)}, u32[]{:S(2)}) async-start(bf16[32,32,128]{2,1,0:T(8,128)(2,1)} %ssd.1), calls=%async_computation.1 | async-start | bytes 524288 | tf_op jit(solution)/shard_map/all_to_all | solution.py:299
  151.3 0.0 copy-done.1
  151.4 2.6 %collective-permute-start.1 = (bf16[64,512]{1,0:T(8,128)(2,1)S(1)}, bf16[64,512]{1,0:T(8,128)(2,1)S(1)}, u32[]{:S(2)}, u32[]{:S(2)}) collective-permute-start(bf16[64,512]{1,0:T(8,128)(2,1)S(1)} %get-tuple-element.2), channel_id=1, source_target_pairs={{0,248},{8,0},{16,240},{24,8},{32,232},{40,16},{48,224},{56,24},{6... | collective-permute-start | bytes 196616 | tf_op jit(solution)/shard_map/ppermute | solution.py:297
  154.0 11.6 %collective-permute-start = (bf16[64,512]{1,0:T(8,128)(2,1)S(1)}, bf16[64,512]{1,0:T(8,128)(2,1)S(1)}, u32[]{:S(2)}, u32[]{:S(2)}) collective-permute-start(bf16[64,512]{1,0:T(8,128)(2,1)S(1)} %get-tuple-element.3), channel_id=1, source_target_pairs={{0,0},{8,248},{16,8},{24,240},{32,16},{40,232},{48,24},{56,224},{6... | collective-permute-start | bytes 196616 | tf_op jit(solution)/shard_map/ppermute | solution.py:297
  165.6 0.0 collective-permute-done.1.q1_ref
  165.6 0.0 copy-start.2
  165.6 1.6 collective-permute-done.q0_ref
  167.2 0.0 copy-done.2
  167.2 0.0 copy-start.3
  167.2 0.6 copy-done.3
  167.9 4.9 %attend.1 = bf16[128,512]{1,0:T(8,128)(2,1)} custom-call(bf16[64,512]{1,0:T(8,128)(2,1)} %copy-done.3, bf16[64,512]{1,0:T(8,128)(2,1)} %copy-done.2, bf16[32,528,128]{2,1,0:T(8,128)(2,1)} %bitcast.3), custom_call_target="tpu_custom_call" | custom-call | flops 1073741824 | bytes 2162688 | tf_op jit(solution)/shard_map/attend/pallas_call | solution.py:244
  172.7 0.7 all-to-all-done.1.g_ref
  173.4 0.0 copy-start
  173.4 0.7 copy-done
  174.1 2.0 %norm.1 = bf16[128,1024]{1,0:T(8,128)(2,1)} custom-call(bf16[32,32,128]{2,1,0:T(8,128)(2,1)} %copy-done, f32[1,1024]{1,0:T(1,128)} %bitcast.4), custom_call_target="tpu_custom_call" | custom-call | flops 1000000 | bytes 524288 | tf_op jit(solution)/shard_map/norm/pallas_call | solution.py:275
  (1 shorter events, 0.0 us)
Async XLA Ops:
  7.2 144.1 %copy-start.1 = (bf16[128,512]{1,0:T(8,128)(2,1)S(1)}, bf16[128,512]{1,0:T(8,128)(2,1)}, u32[]{:S(2)}) copy-start(bf16[128,512]{1,0:T(8,128)(2,1)} %param.12) | copy-start | bytes 393220
  7.2 125.4 %all-gather.3.cloned.1.call-start = ((), (), s32[]{:S(2)}) async-start(), calls=%async_computation.2 | async-start | bytes 4460544 | tf_op jit(solution)/shard_map/all_gather | solution.py:288
  143.2 30.3 %all-to-all-start.1 = ((bf16[32,32,128]{2,1,0:T(8,128)(2,1)}), bf16[32,32,128]{2,1,0:T(8,128)(2,1)S(1)}, u32[]{:S(2)}, u32[]{:S(2)}) async-start(bf16[32,32,128]{2,1,0:T(8,128)(2,1)} %ssd.1), calls=%async_computation.1 | async-start | bytes 524288 | tf_op jit(solution)/shard_map/all_to_all | solution.py:299
  151.4 14.3 %collective-permute-start.1 = (bf16[64,512]{1,0:T(8,128)(2,1)S(1)}, bf16[64,512]{1,0:T(8,128)(2,1)S(1)}, u32[]{:S(2)}, u32[]{:S(2)}) collective-permute-start(bf16[64,512]{1,0:T(8,128)(2,1)S(1)} %get-tuple-element.2), channel_id=1, source_target_pairs={{0,248},{8,0},{16,240},{24,8},{32,232},{40,16},{48,224},{56,24},{6... | collective-permute-start | bytes 196616 | tf_op jit(solution)/shard_map/ppermute | solution.py:297
  154.0 13.2 %collective-permute-start = (bf16[64,512]{1,0:T(8,128)(2,1)S(1)}, bf16[64,512]{1,0:T(8,128)(2,1)S(1)}, u32[]{:S(2)}, u32[]{:S(2)}) collective-permute-start(bf16[64,512]{1,0:T(8,128)(2,1)S(1)} %get-tuple-element.3), channel_id=1, source_target_pairs={{0,0},{8,248},{16,8},{24,240},{32,16},{40,232},{48,24},{56,224},{6... | collective-permute-start | bytes 196616 | tf_op jit(solution)/shard_map/ppermute | solution.py:297
  165.6 1.6 copy-start.2
  167.2 0.6 copy-start.3
  173.4 0.7 copy-start
Sparse Core Ops, SparseCore 0:
  10.7 121.8 all-gather.2

commit v2 on v1

v2 whole, which is shorter than its diff:
```python
import functools
import math

import jax
import jax.numpy as jnp
from jax import lax
from jax.experimental import pallas as pl
from jax.experimental.pallas import tpu as pltpu
from jax.sharding import PartitionSpec as P


HEAD_SIZE = 128
MP = 64
MN = 128
HALF = 64
TOK = 128
CTX = "ctx"
GRP_CTX = ("grp", "ctx")

norm_eps = 1e-05
F32 = jnp.float32
BF16 = jnp.bfloat16
NT = (((1,), (1,)), ((), ()))
TN = (((0,), (0,)), ((), ()))


SMALL = pltpu.CompilerParams(vmem_limit_bytes=16 * 2**20)


def vmem_spec():
    return pl.BlockSpec(memory_space=pltpu.VMEM)


def cost(flops, moved):
    return pl.CostEstimate(flops=flops, bytes_accessed=moved, transcendentals=0)


def is_first_core():
    return lax.rem(lax.axis_index(CTX), 2) == 0


def hbm_spec():
    return pl.BlockSpec(memory_space=pltpu.HBM)


def run_copies(pairs, sems):
    copies = [pltpu.make_async_copy(source, target, sems.at[i]) for i, (source, target) in enumerate(pairs)]
    for copy in copies:
        copy.start()
    return copies


def pack_kernel(k_ref, v_ref, out_ref, sems):
    for copy in run_copies([(k_ref, out_ref.at[:TOK]), (v_ref, out_ref.at[TOK:])], sems):
        copy.wait()


def pack(keys, values):
    return pl.pallas_call(
        pack_kernel,
        out_shape=jax.ShapeDtypeStruct((2 * TOK, HEAD_SIZE), BF16),
        in_specs=[hbm_spec()] * 2,
        out_specs=vmem_spec(),
        scratch_shapes=[pltpu.SemaphoreType.DMA((2,))],
        cost_estimate=cost(10**6, 8 * TOK * TOK),
        name="pack",
    )(keys, values)


def halves_kernel(
    x_ref, z_ref, b_ref, c_ref, dt_ref, bias_ref, alog_ref, skip_ref, mine_ref, theirs_ref, coef_ref, small, sems
):
    half = x_ref.shape[1] // 2
    tiles = half // 128
    heads = bias_ref.shape[0] // 2
    first = is_first_core()
    pairs = [(ref, small.at[i]) for i, ref in enumerate((bias_ref, alog_ref, skip_ref))]
    for out_ref, low in ((theirs_ref, jnp.logical_not(first)), (mine_ref, first)):
        base = jnp.where(low, 0, half)
        for which, ref in enumerate((x_ref, z_ref)):
            for t in range(tiles):
                row = (which * tiles + t) * TOK
                columns = pl.ds(pl.multiple_of(base + t * 128, 128), 128)
                pairs.append((ref.at[:, columns], out_ref.at[row : row + TOK]))
        row = 2 * tiles * TOK
        pairs.append((b_ref, out_ref.at[row : row + TOK]))
        pairs.append((c_ref, out_ref.at[row + TOK : row + 2 * TOK]))
        pairs.append((dt_ref, out_ref.at[row + 2 * TOK :]))
    copies = run_copies(pairs, sems)
    for copy in copies[:3]:
        copy.wait()
    head_row = lax.broadcasted_iota(jnp.int32, (heads, TOK), 0)
    at = jnp.where(first, 0, heads)
    bias, rate, skip = [jnp.zeros((heads, TOK), F32)] * 3
    for h in range(heads):
        bias = jnp.where(head_row == h, small[0, at + h], bias)
        rate = jnp.where(head_row == h, small[1, at + h], rate)
        skip = jnp.where(head_row == h, small[2, at + h], skip)
    rate = jnp.exp(rate)
    coef_ref[...] = jnp.concatenate([bias, bias, rate, rate, skip], axis=0)
    for copy in copies[3:]:
        copy.wait()


def halves(m_x, m_z, m_b, m_c, dt_turned, dt_bias, a_log, d_skip):
    rows = (m_x.shape[1] // 128 + 2) * TOK + dt_turned.shape[0]
    heads = dt_bias.shape[0] // 2
    tiles = m_x.shape[1] // 256
    shape = jax.ShapeDtypeStruct((rows, TOK), BF16)
    return pl.pallas_call(
        halves_kernel,
        out_shape=(shape, shape, jax.ShapeDtypeStruct((5 * heads, TOK), F32)),
        in_specs=[hbm_spec()] * 8,
        out_specs=(vmem_spec(),) * 3,
        scratch_shapes=[
            pltpu.SMEM((3, 2 * heads), F32),
            pltpu.SemaphoreType.DMA((3 + 2 * (2 * tiles + 3),)),
        ],
        cost_estimate=cost(10**6, 8 * rows * TOK),
        name="halves",
    )(m_x, m_z, m_b, m_c, dt_turned, dt_bias, a_log, d_skip)


def pair_of(mine_ref, got_ref, first, row):
    mine, got = mine_ref[row : row + TOK, :], got_ref[row : row + TOK, :]
    one, two = jnp.where(first, mine, got), jnp.where(first, got, mine)
    return (
        jnp.concatenate([one[:HALF], two[:HALF]], axis=0),
        jnp.concatenate([two[HALF:], one[HALF:]], axis=0),
    )


def softplus(v):
    return jnp.maximum(v, 0.0) + jnp.log1p(jnp.exp(-jnp.abs(v)))


def local_kernel(mine_ref, got_ref, coef_ref, states_ref, inner_ref, grown_ref):
    heads = coef_ref.shape[0] // 5
    tiles = heads * MP // 128
    first = is_first_core()
    row = 2 * tiles * TOK
    b_runs = pair_of(mine_ref, got_ref, first, row)
    c_runs = pair_of(mine_ref, got_ref, first, row + TOK)

    lane = lax.broadcasted_iota(jnp.int32, (heads, TOK), 1)
    low = lane < HALF
    mine_dt, got_dt = mine_ref[row + 2 * TOK :, :].astype(F32), got_ref[row + 2 * TOK :, :].astype(F32)
    mine_dt = jnp.where(first, mine_dt[:heads], mine_dt[heads:])
    got_dt = jnp.where(first, got_dt[:heads], got_dt[heads:])
    one, two = jnp.where(first, mine_dt, got_dt), jnp.where(first, got_dt, mine_dt)
    two = pltpu.roll(two, HALF, 1)
    raw = jnp.concatenate([jnp.where(low, one, two), jnp.where(low, two, one)], axis=0)
    bias, rate = coef_ref[: 2 * heads, :], coef_ref[2 * heads : 4 * heads, :]
    dt = softplus(raw + bias)
    run = -dt * rate
    lanes = lax.broadcasted_iota(jnp.int32, (2 * heads, TOK), 1)
    shift = 1
    while shift < TOK:
        run = run + jnp.where(lanes >= shift, pltpu.roll(run, shift, 1), 0.0)
        shift *= 2
    last = jnp.broadcast_to(run[:, TOK - 1 :], run.shape)
    tail = jnp.exp(last - run) * dt
    columns = jnp.concatenate([run, tail, jnp.zeros((TOK - 4 * heads, TOK), F32)], axis=0).T
    grown_ref[...] = jnp.exp(columns[:, : 2 * heads])
    high = last.astype(BF16)
    middle = (last - high.astype(F32)).astype(BF16)
    least = (last - high.astype(F32) - middle.astype(F32)).astype(BF16)
    parts = [part.astype(F32) for part in (high, middle, least)]

    row_id = lax.broadcasted_iota(jnp.int32, (TOK, TOK), 0)
    col_id = lax.broadcasted_iota(jnp.int32, (TOK, TOK), 1)
    seen = row_id >= col_id
    left = col_id < MP
    crosses = [lax.dot_general(c_runs[q], b_runs[q], NT, preferred_element_type=F32) for q in range(2)]
    for t in range(tiles):
        x_runs = pair_of(mine_ref, got_ref, first, t * TOK)
        for q in range(2):
            at = q * heads + 2 * t
            x = x_runs[q]
            wide = x.astype(F32)
            weights = []
            for e in range(2):
                spread = columns[:, at + e : at + e + 1] - run[at + e : at + e + 1, :]
                decay = jnp.exp(jnp.where(seen, spread, -jnp.inf))
                weights.append((crosses[q] * decay * dt[at + e : at + e + 1, :]).astype(BF16))
            both = jnp.dot(jnp.concatenate(weights, axis=0), x, preferred_element_type=F32)
            skip_row = 4 * heads + 2 * t
            skip = jnp.where(left, coef_ref[skip_row : skip_row + 1, :], coef_ref[skip_row + 1 : skip_row + 2, :])
            inner_ref[q, t] = jnp.where(left, both[:TOK], both[TOK:]) + skip * wide
            offset = 2 * heads + at
            tails = jnp.where(left, columns[:, offset : offset + 1], columns[:, offset + 1 : offset + 2])
            state = lax.dot_general((wide * tails).astype(BF16), b_runs[q], TN, preferred_element_type=F32)
            state = state.astype(BF16)
            for piece in range(4):
                states_ref[4 * t + piece, q * 32 : q * 32 + 32, :] = state[piece * 32 : piece * 32 + 32, :]
    part_row = lax.broadcasted_iota(jnp.int32, (8, TOK), 0)
    for h in range(heads):
        block = jnp.zeros((8, TOK), F32)
        for q in range(2):
            at = q * heads + h
            for i in range(3):
                block = jnp.where(part_row == 3 * q + i, parts[i][at : at + 1, :], block)
        for piece in range(2):
            states_ref[2 * h + piece, 64:72, :] = block.astype(BF16)


def local_states(mine, got, coef):
    heads = coef.shape[0] // 5
    width = heads * MP
    return pl.pallas_call(
        local_kernel,
        out_shape=(
            jax.ShapeDtypeStruct((width // 32, 72, MN), BF16),
            jax.ShapeDtypeStruct((2, width // 128, TOK, 128), F32),
            jax.ShapeDtypeStruct((TOK, 2 * heads), F32),
        ),
        in_specs=[vmem_spec()] * 3,
        out_specs=(vmem_spec(), vmem_spec(), vmem_spec()),
        compiler_params=SMALL,
        cost_estimate=cost(10**9, 10**6),
        name="local",
    )(mine, got, coef)


def chain_kernel(states_ref, out_ref):
    count = states_ref.shape[0]
    state = jnp.zeros((32, MN), F32)
    for q in range(2):
        for k in range(count) if q == 0 else reversed(range(count)):
            out_ref[k, q * 32 : q * 32 + 32, :] = state.astype(BF16)
            parts = states_ref[k, 64:72, :].astype(F32)
            decay = jnp.exp(parts[3 * q : 3 * q + 1] + parts[3 * q + 1 : 3 * q + 2] + parts[3 * q + 2 : 3 * q + 3])
            state = state * decay + states_ref[k, q * 32 : q * 32 + 32, :].astype(F32)


def chain(states):
    count = states.shape[0]
    return pl.pallas_call(
        chain_kernel,
        out_shape=jax.ShapeDtypeStruct((count, 64, MN), BF16),
        in_specs=[vmem_spec()],
        out_specs=vmem_spec(),
        compiler_params=SMALL,
        cost_estimate=cost(10**6, 10**6),
        name="chain",
    )(states)


def gate_kernel(entering_ref, inner_ref, grown_ref, mine_ref, got_ref, even_ref, odd_ref):
    tiles = inner_ref.shape[1]
    heads = 2 * tiles
    first = is_first_core()
    c_runs = pair_of(mine_ref, got_ref, first, (2 * tiles + 1) * TOK)
    left = lax.broadcasted_iota(jnp.int32, (TOK, 128), 1) < MP
    for t in range(tiles):
        z_runs = pair_of(mine_ref, got_ref, first, (tiles + t) * TOK)
        results = []
        for q in range(2):
            at = q * heads + 2 * t
            state = entering_ref[4 * t : 4 * t + 4, q * 32 : q * 32 + 32, :].reshape(128, MN)
            carried = lax.dot_general(c_runs[q], state, NT, preferred_element_type=F32)
            grown = jnp.where(left, grown_ref[:, at : at + 1], grown_ref[:, at + 1 : at + 2])
            y = inner_ref[q, t] + carried * grown
            z = z_runs[q].astype(F32)
            results.append((y * (z / (1.0 + jnp.exp(-z)))).astype(BF16))
        even_ref[:, t * 128 : t * 128 + 128] = jnp.where(first, results[0], results[1])
        odd_ref[:, t * 128 : t * 128 + 128] = jnp.where(first, results[1], results[0])


def gate(entering, inner, grown, mine, got):
    shape = jax.ShapeDtypeStruct((TOK, inner.shape[1] * 128), BF16)
    return pl.pallas_call(
        gate_kernel,
        out_shape=(shape, shape),
        in_specs=[vmem_spec()] * 5,
        out_specs=(vmem_spec(), vmem_spec()),
        compiler_params=SMALL,
        cost_estimate=cost(10**8, 10**6),
        name="gate",
    )(entering, inner, grown, mine, got)


def norm_kernel(half_count, even_ref, odd_ref, gain_ref, out_ref):
    early = lax.axis_index(CTX) < half_count
    width = even_ref.shape[1]
    even, odd = even_ref[...], odd_ref[...]
    one = jnp.where(early, even, odd).astype(F32)
    two = jnp.where(early, odd, even).astype(F32)
    power = jnp.sum(one * one + two * two, axis=1, keepdims=True) * (0.5 / width)
    scale = lax.rsqrt(power + norm_eps)
    out_ref[:, :width] = ((one * scale) * gain_ref[:, :width]).astype(BF16)
    out_ref[:, width:] = ((two * scale) * gain_ref[:, width:]).astype(BF16)


def gated_norm(even, odd, gain, half_count):
    return pl.pallas_call(
        functools.partial(norm_kernel, half_count),
        out_shape=jax.ShapeDtypeStruct((TOK, 2 * even.shape[1]), BF16),
        in_specs=[vmem_spec()] * 3,
        out_specs=vmem_spec(),
        compiler_params=SMALL,
        cost_estimate=cost(10**6, 10**6),
        name="norm",
    )(even, odd, gain.reshape(1, -1))


def attend_kernel(count, q0_ref, q1_ref, g_ref, out_ref, kv, q_s, m_s, l_s, acc_s, sems):
    blocks = 8
    parts = count // blocks
    copies = run_copies(
        [(g_ref.at[part * blocks : (part + 1) * blocks], kv.at[part * blocks : (part + 1) * blocks]) for part in range(parts)],
        sems,
    )
    heads = q0_ref.shape[1] // HEAD_SIZE
    for h in range(heads):
        columns = slice(h * HEAD_SIZE, (h + 1) * HEAD_SIZE)
        q_s[h * TOK : h * TOK + HALF, :] = q0_ref[:, columns]
        q_s[h * TOK + HALF : (h + 1) * TOK, :] = q1_ref[:, columns]
    m_s[...] = jnp.full(m_s.shape, -1e30, F32)
    l_s[...] = jnp.zeros(l_s.shape, F32)
    acc_s[...] = jnp.zeros(acc_s.shape, F32)
    me = lax.axis_index(CTX)
    scale = math.log2(math.e) / math.sqrt(HEAD_SIZE)
    rows = heads * TOK
    keys_here = blocks * HALF

    def step(index, masked):
        def piece(offset):
            parts = []
            for p in range(blocks):
                c = index * blocks + p
                early = c < count
                source = jnp.where(early, c, 2 * count - 1 - c)
                start = pl.multiple_of(jnp.where(early, 0, HALF) + offset, HALF)
                parts.append(kv[source, pl.ds(start, HALF), :])
            return jnp.concatenate(parts, axis=0)

        k_rows, v_rows = piece(0), piece(TOK)
        scores = lax.dot_general(k_rows, q_s[...], NT, preferred_element_type=F32)
        if masked:
            key_pos = index * keys_here + lax.broadcasted_iota(jnp.int32, (keys_here, rows), 0)
            column = lax.broadcasted_iota(jnp.int32, (keys_here, rows), 1)
            query_pos = me * TOK + jnp.bitwise_and(column, TOK - 1)
            scores = jnp.where(key_pos <= query_pos, scores, -1e30)
        old = m_s[...]
        new = jnp.maximum(old, jnp.max(scores, axis=0, keepdims=True))
        expons = jnp.exp2((scores - new) * scale)
        if masked:
            expons = jnp.where(key_pos <= query_pos, expons, 0.0)
        factor = jnp.exp2((old - new) * scale)
        m_s[...] = new
        l_s[...] = l_s[...] * factor + jnp.sum(expons, axis=0, keepdims=True)
        acc_s[...] = acc_s[...] * factor + lax.dot_general(
            v_rows, expons.astype(BF16), TN, preferred_element_type=F32
        )

    full = (me * TOK) // keys_here

    def arrived(index):
        for part in range(parts):

            @pl.when(index == part)
            def _():
                copies[part].wait()

    def whole_step(index, _):
        arrived(index)
        step(index, False)

    lax.fori_loop(0, full, whole_step, None)
    arrived(full)
    step(full, True)
    for part in range(parts):

        @pl.when(full < part)
        def _():
            copies[part].wait()

    result = acc_s[...] / l_s[...]
    for h in range(heads):
        columns = slice(h * TOK, (h + 1) * TOK)
        out_ref[:, h * HEAD_SIZE : (h + 1) * HEAD_SIZE] = result[:, columns].T.astype(BF16)


def attend(q0, q1, gathered):
    count, rows, _ = gathered.shape
    heads = q0.shape[1] // HEAD_SIZE
    return pl.pallas_call(
        functools.partial(attend_kernel, count),
        out_shape=jax.ShapeDtypeStruct((TOK, q0.shape[1]), BF16),
        in_specs=[vmem_spec(), vmem_spec(), hbm_spec()],
        out_specs=vmem_spec(),
        scratch_shapes=[
            pltpu.VMEM((count, rows, TOK), BF16),
            pltpu.VMEM((heads * TOK, HEAD_SIZE), BF16),
            pltpu.VMEM((1, heads * TOK), F32),
            pltpu.VMEM((1, heads * TOK), F32),
            pltpu.VMEM((HEAD_SIZE, heads * TOK), F32),
            pltpu.SemaphoreType.DMA((count // 8,)),
        ],
        cost_estimate=cost(4 * heads * TOK * count * TOK * HEAD_SIZE, count * rows * TOK),
        name="attend",
    )(q0, q1, gathered)


def permute(value, count, target):
    return lax.ppermute(value, CTX, [(d, target(d)) for d in range(count)])


def layer(query, keys, values, m_x, m_z, m_b, m_c, dt_raw, dt_bias, a_log, d_skip, norm_gain):
    count = lax.axis_size(CTX)
    chips = count // 2
    gathered = lax.all_gather(pack(keys, values), CTX)

    mine, theirs, coef = halves(m_x, m_z, m_b, m_c, dt_raw.T, dt_bias, a_log, d_skip)
    got = permute(theirs, count, lambda d: d ^ 1)
    states, inner, grown = local_states(mine, got, coef)
    same_core = [list(range(core, count, 2)) for core in range(2)]
    exchange = functools.partial(
        lax.all_to_all, axis_name=CTX, split_axis=0, concat_axis=0, tiled=True, axis_index_groups=same_core
    )
    parity = lax.rem(lax.axis_index(CTX), 2)
    block = [lambda d: d if d % 2 == 0 else 2 * count - 1 - d, lambda d: 2 * count - 1 - d if d % 2 == 0 else d]
    queries = []
    for slot in range(2):
        start = (parity if slot == 0 else 1 - parity) * HALF
        piece = lax.dynamic_slice_in_dim(query, start, HALF, 0)
        queries.append(permute(piece, count, lambda d: block[slot](d) // 2))
    exchanged = exchange(states)
    entering = exchange(chain(exchanged))

    even, odd = gate(entering, inner, grown, mine, got)
    even = permute(even, count, lambda d: d // 2 if d % 2 == 0 else count - 1 - d // 2)
    odd = permute(odd, count, lambda d: count - 1 - d // 2 if d % 2 == 0 else d // 2)
    context = attend(queries[0], queries[1], gathered)
    even, odd, context = lax.optimization_barrier((even, odd, context))
    mixed = gated_norm(even, odd, norm_gain, chips)
    return (context, mixed)


def solution(mesh):
    rows, heads = P(GRP_CTX, "hd"), P("hd")
    return jax.shard_map(
        layer,
        mesh=mesh,
        in_specs=(rows,) * 8 + (heads,) * 4,
        out_specs=(rows, rows),
        check_vma=False,
    )
```

time: 186 us -> 154 us (0.83)
  the two profiles are of different devices: /device:TPU:65 before, /device:TPU:833 now
where the time goes in v2:
time: 154 us; the launch traced here: 153 us
  blocking collectives  45.1 us (29%)
  waiting for transfers between devices  44.3 us (29%)
  starting transfers between devices  35 us (23%)
  between operations  14.2 us (9%)
  Pallas kernels  13 us (8%)
  local copies, waits for them, and re-layouts  1.74 us (1%)
    all_to_all x1, blocking collectives, layer(): exchanged = exchange(states)  45.1 us
    all_gather x1, waiting for transfers between devices, layer(): gathered = lax.all_gather(pack(keys, values), CTX)  37.2 us
    ppermute x5, starting transfers between devices, permute(): return lax.ppermute(value, CTX, [(d, target(d)) for d in range(count)])  24.6 us
    all_to_all x1, starting transfers between devices, layer(): entering = exchange(chain(exchanged))  10.4 us
    pallas_call x1, Pallas kernels, attend(): pl.pallas_call(functools.partial(attend_kernel, count), out_shape=jax.Sha...  5.55 us
    ppermute x5, waiting for transfers between devices, permute(): return lax.ppermute(value, CTX, [(d, target(d)) for d in range(count)])  4.15 us
  transfers between devices with their start and end apart: 7, of which 5 were waited for; matrix products, arithmetic and copies ran while one was open for 0% of the time, Pallas kernels for 7%

profile of v2, /device:TPU:833, one launch (start us, length us, event | category | flops | bytes accessed | tf_op | source)
XLA Modules:
  0.0 153.4 jit_solution(13515909621796956650)
XLA Ops:
  7.2 0.1 all-gather.3.cloned.1.call-start
  7.2 1.4 pack.1
  8.7 0.1 all-gather.3.cloned.1.call-update
  8.7 2.2 %halves.1 = (bf16[1296,128]{1,0:T(8,128)(2,1)}, bf16[1296,128]{1,0:T(8,128)(2,1)}, f32[40,128]{1,0:T(8,128)}) custom-call(bf16[128,1024]{1,0:T(8,128)(2,1)} %x_ref.1, bf16[128,1024]{1,0:T(8,128)(2,1)} %z_ref.1, bf16[128,128]{1,0:T(8,128)(2,1)} %b_ref.1, bf16[128,128]{1,0:T(8,128)(2,1)} %c_ref.1, bf16[16,128]{1,0:T(8,128)(2,1)} %bitcast.4, f32[16]{0:T(128)} %bias_ref.1, ...), custom_call_target="tpu_custom_call" | custom-call | flops 1000000 | bytes 1327104 | tf_op jit(solution)/shard_map/halves/pallas_call | solution.py:110
  10.9 2.5 %collective-permute-start = (bf16[1296,128]{1,0:T(8,128)(2,1)}, bf16[1296,128]{1,0:T(8,128)(2,1)S(1)}, u32[]{:S(2)}, u32[]{:S(2)}) collective-permute-start(bf16[1296,128]{1,0:T(8,128)(2,1)} %get-tuple-element.14), channel_id=1, source_target_pairs={{0,8},{8,0},{16,24},{24,16},{32,40},{40,32},{48,56},{56,48},{64,72... | collective-permute-start | bytes 995336 | tf_op jit(solution)/shard_map/ppermute | solution.py:407
  13.5 1.4 collective-permute-done.got_ref
  14.9 1.0 copy-done
  15.9 0.0 copy-start.3
  15.9 0.7 copy-done.3
  16.6 1.8 %local.1 = (bf16[16,72,128]{2,1,0:T(8,128)(2,1)S(1)}, f32[2,4,128,128]{3,2,1,0:T(8,128)S(1)}, f32[128,16]{1,0:T(8,128)S(1)}) custom-call(bf16[1296,128]{1,0:T(8,128)(2,1)S(1)} %copy-done, bf16[1296,128]{1,0:T(8,128)(2,1)S(1)} %collective-permute-done.got_ref, f32[40,128]{1,0:T(8,128)S(1)} %copy-done.3), custom_call_target="tpu_custom_call" | custom-call | flops 1000000000 | bytes 1000000 | tf_op jit(solution)/shard_map/local/pallas_call | solution.py:210
  18.4 45.1 %all_to_all.10.states_ref = bf16[16,72,128]{2,1,0:T(8,128)(2,1)S(1)} all-to-all(bf16[16,72,128]{2,1,0:T(8,128)(2,1)S(1)} %get-tuple-element.16), channel_id=1, replica_groups={{0,16,32,48,64,80,96,112,128,144,160,176,192,208,224,240},{8,24,40,56,7..., dimensions={0} | all-to-all | bytes 589824 | tf_op jit(solution)/shard_map/all_to_all | solution.py:429
  63.5 0.8 chain.1
  64.3 10.4 %all-to-all-start.1 = ((bf16[16,64,128]{2,1,0:T(8,128)(2,1)}), bf16[16,64,128]{2,1,0:T(8,128)(2,1)S(1)}, u32[]{:S(2)}, u32[]{:S(2)}) async-start(bf16[16,64,128]{2,1,0:T(8,128)(2,1)} %chain.1), calls=%async_computation.1 | async-start | bytes 524288 | tf_op jit(solution)/shard_map/all_to_all | solution.py:430
  74.7 0.0 copy-done.4
  74.7 3.3 %collective-permute-start.4 = (bf16[64,512]{1,0:T(8,128)(2,1)S(1)}, bf16[64,512]{1,0:T(8,128)(2,1)S(1)}, u32[]{:S(2)}, u32[]{:S(2)}) collective-permute-start(bf16[64,512]{1,0:T(8,128)(2,1)S(1)} %get-tuple-element.24), channel_id=1, source_target_pairs={{0,248},{8,0},{16,240},{24,8},{32,232},{40,16},{48,224},{56,24},{6... | collective-permute-start | bytes 196616 | tf_op jit(solution)/shard_map/ppermute | solution.py:407
  78.0 10.0 %collective-permute-start.3 = (bf16[64,512]{1,0:T(8,128)(2,1)S(1)}, bf16[64,512]{1,0:T(8,128)(2,1)S(1)}, u32[]{:S(2)}, u32[]{:S(2)}) collective-permute-start(bf16[64,512]{1,0:T(8,128)(2,1)S(1)} %get-tuple-element.25), channel_id=1, source_target_pairs={{0,0},{8,248},{16,8},{24,240},{32,16},{40,232},{48,24},{56,224},{6... | collective-permute-start | bytes 196616 | tf_op jit(solution)/shard_map/ppermute | solution.py:407
  88.1 2.9 %all-to-all-done.1.entering_ref = bf16[16,64,128]{2,1,0:T(8,128)(2,1)S(1)} async-done(((bf16[16,64,128]{2,1,0:T(8,128)(2,1)}), bf16[16,64,128]{2,1,0:T(8,128)(2,1)S(1)}, u32[]{:S(2)}, u32[]{:S(2)}) %all-to-all-start.1) | async-done | bytes 262176 | tf_op jit(solution)/shard_map/all_to_all | solution.py:430
  91.0 0.0 copy-done.1
  91.0 0.4 gate.1
  91.4 0.0 copy-start.2
  91.4 6.0 %collective-permute-start.1 = (bf16[128,512]{1,0:T(8,128)(2,1)S(1)}, bf16[128,512]{1,0:T(8,128)(2,1)S(1)}, u32[]{:S(2)}, u32[]{:S(2)}) collective-permute-start(bf16[128,512]{1,0:T(8,128)(2,1)S(1)} %get-tuple-element.19), channel_id=1, source_target_pairs={{0,0},{8,248},{16,8},{24,240},{32,16},{40,232},{48,24},{56,224},{6... | collective-permute-start | bytes 393224 | tf_op jit(solution)/shard_map/ppermute | solution.py:407
  97.4 2.8 %collective-permute-start.2 = (bf16[128,512]{1,0:T(8,128)(2,1)S(1)}, bf16[128,512]{1,0:T(8,128)(2,1)S(1)}, u32[]{:S(2)}, u32[]{:S(2)}) collective-permute-start(bf16[128,512]{1,0:T(8,128)(2,1)S(1)} %get-tuple-element.20), channel_id=1, source_target_pairs={{0,248},{8,0},{16,240},{24,8},{32,232},{40,16},{48,224},{56,24},{6... | collective-permute-start | bytes 393224 | tf_op jit(solution)/shard_map/ppermute | solution.py:407
  100.2 0.7 collective-permute-done.4.q1_ref
  100.8 2.0 %collective-permute-done.3.q0_ref = bf16[64,512]{1,0:T(8,128)(2,1)S(1)} collective-permute-done((bf16[64,512]{1,0:T(8,128)(2,1)S(1)}, bf16[64,512]{1,0:T(8,128)(2,1)S(1)}, u32[]{:S(2)}, u32[]{:S(2)}) %collective-permute-start.3) | collective-permute-done | bytes 65568 | tf_op jit(solution)/shard_map/ppermute | solution.py:407
  102.9 37.2 %all-gather.3.cloned.1.call-done = bf16[8192,128]{1,0:T(8,128)(2,1)} async-done(((bf16[256,128]{1,0:T(8,128)(2,1)}), bf16[8192,128]{1,0:T(8,128)(2,1)}) %all-gather.3.cloned.1.call-update) | async-done | bytes 2097168 | tf_op jit(solution)/shard_map/all_gather | solution.py:413
  140.1 0.0 copy-done.5
  140.1 0.0 copy-done.6
  140.1 5.6 %attend.1 = bf16[128,512]{1,0:T(8,128)(2,1)} custom-call(bf16[64,512]{1,0:T(8,128)(2,1)} %copy-done.6, bf16[64,512]{1,0:T(8,128)(2,1)} %copy-done.5, bf16[32,256,128]{2,1,0:T(8,128)(2,1)} %bitcast.5), custom_call_target="tpu_custom_call" | custom-call | flops 1073741824 | bytes 1048576 | tf_op jit(solution)/shard_map/attend/pallas_call | solution.py:388
  145.6 0.0 collective-permute-done.1.even_ref
  145.6 0.0 collective-permute-done.2.odd_ref
  145.6 0.0 copy-done.2
  145.7 0.9 norm.1
  (6 shorter events, 0.0 us)
Async XLA Ops:
  7.2 132.9 %all-gather.3.cloned.1.call-start = ((), (), s32[]{:S(2)}) async-start(), calls=%async_computation.2 | async-start | bytes 2162688 | tf_op jit(solution)/shard_map/all_gather | solution.py:413
  10.9 4.0 %collective-permute-start = (bf16[1296,128]{1,0:T(8,128)(2,1)}, bf16[1296,128]{1,0:T(8,128)(2,1)S(1)}, u32[]{:S(2)}, u32[]{:S(2)}) collective-permute-start(bf16[1296,128]{1,0:T(8,128)(2,1)} %get-tuple-element.14), channel_id=1, source_target_pairs={{0,8},{8,0},{16,24},{24,16},{32,40},{40,32},{48,56},{56,48},{64,72... | collective-permute-start | bytes 995336 | tf_op jit(solution)/shard_map/ppermute | solution.py:407
  14.9 1.0 copy-start
  15.9 0.7 copy-start.3
  16.6 58.1 %copy-start.4 = (bf16[128,512]{1,0:T(8,128)(2,1)S(1)}, bf16[128,512]{1,0:T(8,128)(2,1)}, u32[]{:S(2)}) copy-start(bf16[128,512]{1,0:T(8,128)(2,1)} %param.12) | copy-start | bytes 393220
  16.6 74.4 %copy-start.1 = (bf16[1296,128]{1,0:T(8,128)(2,1)S(1)}, bf16[1296,128]{1,0:T(8,128)(2,1)}, u32[]{:S(2)}) copy-start(bf16[1296,128]{1,0:T(8,128)(2,1)} %get-tuple-element.13.mine_ref) | copy-start | bytes 995332
  64.3 26.7 %all-to-all-start.1 = ((bf16[16,64,128]{2,1,0:T(8,128)(2,1)}), bf16[16,64,128]{2,1,0:T(8,128)(2,1)S(1)}, u32[]{:S(2)}, u32[]{:S(2)}) async-start(bf16[16,64,128]{2,1,0:T(8,128)(2,1)} %chain.1), calls=%async_computation.1 | async-start | bytes 524288 | tf_op jit(solution)/shard_map/all_to_all | solution.py:430
  74.7 26.1 %collective-permute-start.4 = (bf16[64,512]{1,0:T(8,128)(2,1)S(1)}, bf16[64,512]{1,0:T(8,128)(2,1)S(1)}, u32[]{:S(2)}, u32[]{:S(2)}) collective-permute-start(bf16[64,512]{1,0:T(8,128)(2,1)S(1)} %get-tuple-element.24), channel_id=1, source_target_pairs={{0,248},{8,0},{16,240},{24,8},{32,232},{40,16},{48,224},{56,24},{6... | collective-permute-start | bytes 196616 | tf_op jit(solution)/shard_map/ppermute | solution.py:407
  78.0 24.8 %collective-permute-start.3 = (bf16[64,512]{1,0:T(8,128)(2,1)S(1)}, bf16[64,512]{1,0:T(8,128)(2,1)S(1)}, u32[]{:S(2)}, u32[]{:S(2)}) collective-permute-start(bf16[64,512]{1,0:T(8,128)(2,1)S(1)} %get-tuple-element.25), channel_id=1, source_target_pairs={{0,0},{8,248},{16,8},{24,240},{32,16},{40,232},{48,24},{56,224},{6... | collective-permute-start | bytes 196616 | tf_op jit(solution)/shard_map/ppermute | solution.py:407
  91.4 54.2 %copy-start.2 = (f32[1024]{0:T(1024)S(1)}, f32[1024]{0:T(1024)}, u32[]{:S(2)}) copy-start(f32[1024]{0:T(1024)} %param.23) | copy-start | bytes 12292
  91.4 54.2 %collective-permute-start.1 = (bf16[128,512]{1,0:T(8,128)(2,1)S(1)}, bf16[128,512]{1,0:T(8,128)(2,1)S(1)}, u32[]{:S(2)}, u32[]{:S(2)}) collective-permute-start(bf16[128,512]{1,0:T(8,128)(2,1)S(1)} %get-tuple-element.19), channel_id=1, source_target_pairs={{0,0},{8,248},{16,8},{24,240},{32,16},{40,232},{48,24},{56,224},{6... | collective-permute-start | bytes 393224 | tf_op jit(solution)/shard_map/ppermute | solution.py:407
  97.4 48.2 %collective-permute-start.2 = (bf16[128,512]{1,0:T(8,128)(2,1)S(1)}, bf16[128,512]{1,0:T(8,128)(2,1)S(1)}, u32[]{:S(2)}, u32[]{:S(2)}) collective-permute-start(bf16[128,512]{1,0:T(8,128)(2,1)S(1)} %get-tuple-element.20), channel_id=1, source_target_pairs={{0,248},{8,0},{16,240},{24,8},{32,232},{40,16},{48,224},{56,24},{6... | collective-permute-start | bytes 393224 | tf_op jit(solution)/shard_map/ppermute | solution.py:407
  100.8 39.2 %copy-start.5 = (bf16[64,512]{1,0:T(8,128)(2,1)}, bf16[64,512]{1,0:T(8,128)(2,1)S(1)}, u32[]{:S(2)}) copy-start(bf16[64,512]{1,0:T(8,128)(2,1)S(1)} %collective-permute-done.4.q1_ref) | copy-start | bytes 196612
  102.9 37.2 %copy-start.6 = (bf16[64,512]{1,0:T(8,128)(2,1)}, bf16[64,512]{1,0:T(8,128)(2,1)S(1)}, u32[]{:S(2)}) copy-start(bf16[64,512]{1,0:T(8,128)(2,1)S(1)} %collective-permute-done.3.q0_ref) | copy-start | bytes 196612
Sparse Core Ops, SparseCore 0:
  10.7 129.2 all-gather.2

commit v3 on v2

--- a/solution.py
+++ b/solution.py
@@ -50,31 +50,15 @@
     return copies
 
 
-def pack_kernel(k_ref, v_ref, out_ref, sems):
-    for copy in run_copies([(k_ref, out_ref.at[:TOK]), (v_ref, out_ref.at[TOK:])], sems):
-        copy.wait()
-
-
-def pack(keys, values):
-    return pl.pallas_call(
-        pack_kernel,
-        out_shape=jax.ShapeDtypeStruct((2 * TOK, HEAD_SIZE), BF16),
-        in_specs=[hbm_spec()] * 2,
-        out_specs=vmem_spec(),
-        scratch_shapes=[pltpu.SemaphoreType.DMA((2,))],
-        cost_estimate=cost(10**6, 8 * TOK * TOK),
-        name="pack",
-    )(keys, values)
-
-
-def halves_kernel(
-    x_ref, z_ref, b_ref, c_ref, dt_ref, bias_ref, alog_ref, skip_ref, mine_ref, theirs_ref, coef_ref, small, sems
-):
+def halves_kernel(*refs):
+    x_ref, z_ref, b_ref, c_ref, dt_ref, k_ref, v_ref, q_ref, bias_ref, alog_ref, skip_ref = refs[:11]
+    mine_ref, theirs_ref, kv_ref, even_ref, odd_ref, small, sems = refs[11:]
     half = x_ref.shape[1] // 2
     tiles = half // 128
     heads = bias_ref.shape[0] // 2
     first = is_first_core()
     pairs = [(ref, small.at[i]) for i, ref in enumerate((bias_ref, alog_ref, skip_ref))]
+    pairs += [(k_ref, kv_ref.at[:TOK]), (v_ref, kv_ref.at[TOK:])]
     for out_ref, low in ((theirs_ref, jnp.logical_not(first)), (mine_ref, first)):
         base = jnp.where(low, 0, half)
         for which, ref in enumerate((x_ref, z_ref)):
@@ -85,7 +69,10 @@
         row = 2 * tiles * TOK
         pairs.append((b_ref, out_ref.at[row : row + TOK]))
         pairs.append((c_ref, out_ref.at[row + TOK : row + 2 * TOK]))
-        pairs.append((dt_ref, out_ref.at[row + 2 * TOK :]))
+        pairs.append((dt_ref, out_ref.at[row + 2 * TOK : row + 2 * TOK + 2 * heads]))
+    for out_ref, low in ((even_ref, first), (odd_ref, jnp.logical_not(first))):
+        start = pl.multiple_of(jnp.where(low, 0, HALF), HALF)
+        pairs.append((q_ref.at[pl.ds(start, HALF), :], out_ref))
     copies = run_copies(pairs, sems)
     for copy in copies[:3]:
         copy.wait()
@@ -97,28 +84,39 @@
         rate = jnp.where(head_row == h, small[1, at + h], rate)
         skip = jnp.where(head_row == h, small[2, at + h], skip)
     rate = jnp.exp(rate)
-    coef_ref[...] = jnp.concatenate([bias, bias, rate, rate, skip], axis=0)
+    rest = jnp.concatenate([bias, bias, rate, rate, skip, skip], axis=0)
+    start = row + 2 * TOK + 2 * heads
+    for part in range(3):
+        rounded = rest.astype(BF16)
+        mine_ref[start + part * 6 * heads : start + (part + 1) * 6 * heads, :] = rounded
+        rest = rest - rounded.astype(F32)
     for copy in copies[3:]:
         copy.wait()
 
 
-def halves(m_x, m_z, m_b, m_c, dt_turned, dt_bias, a_log, d_skip):
-    rows = (m_x.shape[1] // 128 + 2) * TOK + dt_turned.shape[0]
+def halves(m_x, m_z, m_b, m_c, dt_turned, keys, values, query, dt_bias, a_log, d_skip):
     heads = dt_bias.shape[0] // 2
+    rows = (m_x.shape[1] // 128 + 2) * TOK + 2 * heads
     tiles = m_x.shape[1] // 256
-    shape = jax.ShapeDtypeStruct((rows, TOK), BF16)
+    half_query = jax.ShapeDtypeStruct((HALF, query.shape[1]), BF16)
     return pl.pallas_call(
         halves_kernel,
-        out_shape=(shape, shape, jax.ShapeDtypeStruct((5 * heads, TOK), F32)),
-        in_specs=[hbm_spec()] * 8,
-        out_specs=(vmem_spec(),) * 3,
+        out_shape=(
+            jax.ShapeDtypeStruct((rows + 18 * heads, TOK), BF16),
+            jax.ShapeDtypeStruct((rows, TOK), BF16),
+            jax.ShapeDtypeStruct((2 * TOK, HEAD_SIZE), BF16),
+            half_query,
+            half_query,
+        ),
+        in_specs=[hbm_spec()] * 11,
+        out_specs=(vmem_spec(),) * 5,
         scratch_shapes=[
             pltpu.SMEM((3, 2 * heads), F32),
-            pltpu.SemaphoreType.DMA((3 + 2 * (2 * tiles + 3),)),
+            pltpu.SemaphoreType.DMA((5 + 2 * (2 * tiles + 3) + 2,)),
         ],
         cost_estimate=cost(10**6, 8 * rows * TOK),
         name="halves",
-    )(m_x, m_z, m_b, m_c, dt_turned, dt_bias, a_log, d_skip)
+    )(m_x, m_z, m_b, m_c, dt_turned, keys, values, query, dt_bias, a_log, d_skip)
 
 
 def pair_of(mine_ref, got_ref, first, row):
@@ -134,8 +132,8 @@
     return jnp.maximum(v, 0.0) + jnp.log1p(jnp.exp(-jnp.abs(v)))
 
 
-def local_kernel(mine_ref, got_ref, coef_ref, states_ref, inner_ref, grown_ref):
-    heads = coef_ref.shape[0] // 5
+def local_kernel(mine_ref, got_ref, states_ref, inner_ref, grown_ref):
+    heads = (mine_ref.shape[0] - got_ref.shape[0]) // 18
     tiles = heads * MP // 128
     first = is_first_core()
     row = 2 * tiles * TOK
@@ -144,13 +142,17 @@
 
     lane = lax.broadcasted_iota(jnp.int32, (heads, TOK), 1)
     low = lane < HALF
-    mine_dt, got_dt = mine_ref[row + 2 * TOK :, :].astype(F32), got_ref[row + 2 * TOK :, :].astype(F32)
+    dt_rows = slice(row + 2 * TOK, row + 2 * TOK + 2 * heads)
+    mine_dt, got_dt = mine_ref[dt_rows, :].astype(F32), got_ref[dt_rows, :].astype(F32)
+    coef = sum(
+        mine_ref[dt_rows.stop + part * 6 * heads : dt_rows.stop + (part + 1) * 6 * heads, :].astype(F32) for part in range(3)
+    )
     mine_dt = jnp.where(first, mine_dt[:heads], mine_dt[heads:])
     got_dt = jnp.where(first, got_dt[:heads], got_dt[heads:])
     one, two = jnp.where(first, mine_dt, got_dt), jnp.where(first, got_dt, mine_dt)
     two = pltpu.roll(two, HALF, 1)
     raw = jnp.concatenate([jnp.where(low, one, two), jnp.where(low, two, one)], axis=0)
-    bias, rate = coef_ref[: 2 * heads, :], coef_ref[2 * heads : 4 * heads, :]
+    bias, rate = coef[: 2 * heads, :], coef[2 * heads : 4 * heads, :]
     dt = softplus(raw + bias)
     run = -dt * rate
     lanes = lax.broadcasted_iota(jnp.int32, (2 * heads, TOK), 1)
@@ -185,7 +187,7 @@
                 weights.append((crosses[q] * decay * dt[at + e : at + e + 1, :]).astype(BF16))
             both = jnp.dot(jnp.concatenate(weights, axis=0), x, preferred_element_type=F32)
             skip_row = 4 * heads + 2 * t
-            skip = jnp.where(left, coef_ref[skip_row : skip_row + 1, :], coef_ref[skip_row + 1 : skip_row + 2, :])
+            skip = jnp.where(left, coef[skip_row : skip_row + 1, :], coef[skip_row + 1 : skip_row + 2, :])
             inner_ref[q, t] = jnp.where(left, both[:TOK], both[TOK:]) + skip * wide
             offset = 2 * heads + at
             tails = jnp.where(left, columns[:, offset : offset + 1], columns[:, offset + 1 : offset + 2])
@@ -204,8 +206,8 @@
             states_ref[2 * h + piece, 64:72, :] = block.astype(BF16)
 
 
-def local_states(mine, got, coef):
-    heads = coef.shape[0] // 5
+def local_states(mine, got):
+    heads = (mine.shape[0] - got.shape[0]) // 18
     width = heads * MP
     return pl.pallas_call(
         local_kernel,
@@ -214,12 +216,12 @@
             jax.ShapeDtypeStruct((2, width // 128, TOK, 128), F32),
             jax.ShapeDtypeStruct((TOK, 2 * heads), F32),
         ),
-        in_specs=[vmem_spec()] * 3,
+        in_specs=[vmem_spec()] * 2,
         out_specs=(vmem_spec(), vmem_spec(), vmem_spec()),
         compiler_params=SMALL,
         cost_estimate=cost(10**9, 10**6),
         name="local",
-    )(mine, got, coef)
+    )(mine, got)
 
 
 def chain_kernel(states_ref, out_ref):
@@ -280,10 +282,10 @@
     )(entering, inner, grown, mine, got)
 
 
-def norm_kernel(half_count, even_ref, odd_ref, gain_ref, out_ref):
+def norm_kernel(half_count, even_ref, odd_ref, even_far_ref, odd_far_ref, gain_ref, out_ref):
     early = lax.axis_index(CTX) < half_count
     width = even_ref.shape[1]
-    even, odd = even_ref[...], odd_ref[...]
+    even, odd = even_ref[...] + even_far_ref[...], odd_ref[...] + odd_far_ref[...]
     one = jnp.where(early, even, odd).astype(F32)
     two = jnp.where(early, odd, even).astype(F32)
     power = jnp.sum(one * one + two * two, axis=1, keepdims=True) * (0.5 / width)
@@ -292,25 +294,33 @@
     out_ref[:, width:] = ((two * scale) * gain_ref[:, width:]).astype(BF16)
 
 
-def gated_norm(even, odd, gain, half_count):
+def gated_norm(even, odd, even_far, odd_far, gain, half_count):
     return pl.pallas_call(
         functools.partial(norm_kernel, half_count),
         out_shape=jax.ShapeDtypeStruct((TOK, 2 * even.shape[1]), BF16),
-        in_specs=[vmem_spec()] * 3,
+        in_specs=[vmem_spec()] * 5,
         out_specs=vmem_spec(),
         compiler_params=SMALL,
         cost_estimate=cost(10**6, 10**6),
         name="norm",
-    )(even, odd, gain.reshape(1, -1))
+    )(even, odd, even_far, odd_far, gain.reshape(1, -1))
 
 
 def attend_kernel(count, q0_ref, q1_ref, g_ref, out_ref, kv, q_s, m_s, l_s, acc_s, sems):
     blocks = 8
     parts = count // blocks
-    copies = run_copies(
-        [(g_ref.at[part * blocks : (part + 1) * blocks], kv.at[part * blocks : (part + 1) * blocks]) for part in range(parts)],
-        sems,
-    )
+    me = lax.axis_index(CTX)
+    keys_here = blocks * HALF
+    full = (me * TOK) // keys_here
+    copies = []
+    for part in range(parts):
+        of_part = slice(part * blocks, (part + 1) * blocks)
+        copies.append(pltpu.make_async_copy(g_ref.at[of_part], kv.at[of_part], sems.at[part]))
+
+        @pl.when(part <= full)
+        def _():
+            copies[part].start()
+
     heads = q0_ref.shape[1] // HEAD_SIZE
     for h in range(heads):
         columns = slice(h * HEAD_SIZE, (h + 1) * HEAD_SIZE)
@@ -319,16 +329,14 @@
     m_s[...] = jnp.full(m_s.shape, -1e30, F32)
     l_s[...] = jnp.zeros(l_s.shape, F32)
     acc_s[...] = jnp.zeros(acc_s.shape, F32)
-    me = lax.axis_index(CTX)
     scale = math.log2(math.e) / math.sqrt(HEAD_SIZE)
     rows = heads * TOK
-    keys_here = blocks * HALF
-
-    def step(index, masked):
+
+    def step(first_block, block_count, diagonal):
         def piece(offset):
             parts = []
-            for p in range(blocks):
-                c = index * blocks + p
+            for p in range(block_count):
+                c = first_block + p
                 early = c < count
                 source = jnp.where(early, c, 2 * count - 1 - c)
                 start = pl.multiple_of(jnp.where(early, 0, HALF) + offset, HALF)
@@ -337,16 +345,16 @@
 
         k_rows, v_rows = piece(0), piece(TOK)
         scores = lax.dot_general(k_rows, q_s[...], NT, preferred_element_type=F32)
-        if masked:
-            key_pos = index * keys_here + lax.broadcasted_iota(jnp.int32, (keys_here, rows), 0)
-            column = lax.broadcasted_iota(jnp.int32, (keys_here, rows), 1)
-            query_pos = me * TOK + jnp.bitwise_and(column, TOK - 1)
-            scores = jnp.where(key_pos <= query_pos, scores, -1e30)
+        if diagonal:
+            key = lax.broadcasted_iota(jnp.int32, (TOK, rows), 0)
+            column = lax.broadcasted_iota(jnp.int32, (TOK, rows), 1)
+            seen = key <= jnp.bitwise_and(column, TOK - 1)
+            scores = jnp.where(seen, scores, -1e30)
         old = m_s[...]
         new = jnp.maximum(old, jnp.max(scores, axis=0, keepdims=True))
         expons = jnp.exp2((scores - new) * scale)
-        if masked:
-            expons = jnp.where(key_pos <= query_pos, expons, 0.0)
+        if diagonal:
+            expons = jnp.where(seen, expons, 0.0)
         factor = jnp.exp2((old - new) * scale)
         m_s[...] = new
         l_s[...] = l_s[...] * factor + jnp.sum(expons, axis=0, keepdims=True)
@@ -354,8 +362,6 @@
             v_rows, expons.astype(BF16), TN, preferred_element_type=F32
         )
 
-    full = (me * TOK) // keys_here
-
     def arrived(index):
         for part in range(parts):
 
@@ -365,17 +371,18 @@
 
     def whole_step(index, _):
         arrived(index)
-        step(index, False)
+        step(index * blocks, blocks, False)
 
     lax.fori_loop(0, full, whole_step, None)
     arrived(full)
-    step(full, True)
-    for part in range(parts):
-
-        @pl.when(full < part)
+    left = lax.rem(me * TOK, keys_here) // TOK
+    for whole in range(1, keys_here // TOK):
+
+        @pl.when(left == whole)
         def _():
-            copies[part].wait()
-
+            step(full * blocks, 2 * whole, False)
+
+    step(2 * me, 2, True)
     result = acc_s[...] / l_s[...]
     for h in range(heads):
         columns = slice(h * TOK, (h + 1) * TOK)
@@ -403,38 +410,56 @@
     )(q0, q1, gathered)
 
 
-def permute(value, count, target):
-    return lax.ppermute(value, CTX, [(d, target(d)) for d in range(count)])
+def permute(value, target, sources):
+    return lax.ppermute(value, CTX, [(d, target(d)) for d in sources])
+
+
+RELAY_HOPS = 7
+RESULT_RELAYS = 1
+
+
+def relay(value, count, chips):
+    sources = range(count - 2 * chips, count)
+    return permute(value, lambda d: (d + 2 * RELAY_HOPS) % count, sources)
+
+
+def forward(value, count, chips, target):
+    sources = range(count - 2 * chips, count)
+    return lax.ppermute(value, CTX, [((d + 2 * RELAY_HOPS) % count, target(d)) for d in sources])
 
 
 def layer(query, keys, values, m_x, m_z, m_b, m_c, dt_raw, dt_bias, a_log, d_skip, norm_gain):
     count = lax.axis_size(CTX)
     chips = count // 2
-    gathered = lax.all_gather(pack(keys, values), CTX)
-
-    mine, theirs, coef = halves(m_x, m_z, m_b, m_c, dt_raw.T, dt_bias, a_log, d_skip)
-    got = permute(theirs, count, lambda d: d ^ 1)
-    states, inner, grown = local_states(mine, got, coef)
+    mine, theirs, pairs, *pieces = halves(
+        m_x, m_z, m_b, m_c, dt_raw.T, keys, values, query, dt_bias, a_log, d_skip
+    )
+    gathered = lax.all_gather(pairs, CTX)
+    got = permute(theirs, lambda d: d ^ 1, range(count))
+    states, inner, grown = local_states(mine, got)
     same_core = [list(range(core, count, 2)) for core in range(2)]
     exchange = functools.partial(
         lax.all_to_all, axis_name=CTX, split_axis=0, concat_axis=0, tiled=True, axis_index_groups=same_core
     )
-    parity = lax.rem(lax.axis_index(CTX), 2)
     block = [lambda d: d if d % 2 == 0 else 2 * count - 1 - d, lambda d: 2 * count - 1 - d if d % 2 == 0 else d]
     queries = []
     for slot in range(2):
-        start = (parity if slot == 0 else 1 - parity) * HALF
-        piece = lax.dynamic_slice_in_dim(query, start, HALF, 0)
-        queries.append(permute(piece, count, lambda d: block[slot](d) // 2))
+        queries.append(permute(pieces[slot], lambda d: block[slot](d) // 2, range(count)))
     exchanged = exchange(states)
     entering = exchange(chain(exchanged))
 
     even, odd = gate(entering, inner, grown, mine, got)
-    even = permute(even, count, lambda d: d // 2 if d % 2 == 0 else count - 1 - d // 2)
-    odd = permute(odd, count, lambda d: count - 1 - d // 2 if d % 2 == 0 else d // 2)
+    goals = [
+        lambda d: d // 2 if d % 2 == 0 else count - 1 - d // 2,
+        lambda d: count - 1 - d // 2 if d % 2 == 0 else d // 2,
+    ]
+    results = (even, odd)
+    direct = [permute(results[slot], goals[slot], range(count - 2 * RESULT_RELAYS)) for slot in range(2)]
+    relayed = [relay(results[slot], count, RESULT_RELAYS) for slot in range(2)]
+    ahead = [forward(relayed[slot], count, RESULT_RELAYS, goals[slot]) for slot in range(2)]
     context = attend(queries[0], queries[1], gathered)
-    even, odd, context = lax.optimization_barrier((even, odd, context))
-    mixed = gated_norm(even, odd, norm_gain, chips)
+    direct, ahead, context = lax.optimization_barrier((direct, ahead, context))
+    mixed = gated_norm(*direct, *ahead, norm_gain, chips)
     return (context, mixed)
 
 

time: 154 us -> 156 us (1.013)
  the two profiles are of different devices: /device:TPU:833 before, /device:TPU:724 now
where the time goes in v3:
time: 156 us; the launch traced here: 155 us
  blocking collectives  76.5 us (49%)
  waiting for transfers between devices  30.2 us (19%)
  starting transfers between devices  21.9 us (14%)
  between operations  14.3 us (9%)
  Pallas kernels  10.5 us (7%)
  local copies, waits for them, and re-layouts  1.58 us (1%)
    all_to_all x1, blocking collectives, layer(): exchanged = exchange(states)  50.6 us
    ppermute x7, waiting for transfers between devices, permute(): return lax.ppermute(value, CTX, [(d, target(d)) for d in sources])  30.2 us
    all_to_all x1, blocking collectives, layer(): entering = exchange(chain(exchanged))  26 us
    ppermute x7, starting transfers between devices, permute(): return lax.ppermute(value, CTX, [(d, target(d)) for d in sources])  20.5 us
    pallas_call x1, Pallas kernels, attend(): pl.pallas_call(functools.partial(attend_kernel, count), out_shape=jax.Sha...  4.98 us
  transfers between devices with their start and end apart: 10, of which 3 were waited for; matrix products, arithmetic and copies ran while one was open for 0% of the time, Pallas kernels for 5%

profile of v3, /device:TPU:724, one launch (start us, length us, event | category | flops | bytes accessed | tf_op | source)
XLA Modules:
  0.0 155.1 jit_solution(15274605284603587913)
XLA Ops:
  7.2 0.1 all-gather.3.cloned.1.call-start
  7.2 2.4 %halves.1 = (bf16[1440,128]{1,0:T(8,128)(2,1)}, bf16[1296,128]{1,0:T(8,128)(2,1)}, bf16[256,128]{1,0:T(8,128)(2,1)}, bf16[64,512]{1,0:T(8,128)(2,1)}, bf16[64,512]{1,0:T(8,128)(2,1)}) custom-call(bf16[128,1024]{1,0:T(8,128)(2,1)} %refs_0_.1, bf16[128,1024]{1,0:T(8,128)(2,1)} %refs_1_.1, bf16[128,128]{1,0:T(8,128)(2,1)} %refs_2_.1, bf16[128,128]{1,0:T(8,128)(2,1)} %refs_3_.1, ...), custom_call_target="tpu_custom_call" | custom-call | flops 1000000 | bytes 1327104 | tf_op jit(solution)/shard_map/halves/pallas_call | solution.py:102
  9.6 0.1 all-gather.3.cloned.1.call-update
  9.7 2.0 %collective-permute-start = (bf16[1296,128]{1,0:T(8,128)(2,1)}, bf16[1296,128]{1,0:T(8,128)(2,1)S(1)}, u32[]{:S(2)}, u32[]{:S(2)}) collective-permute-start(bf16[1296,128]{1,0:T(8,128)(2,1)} %get-tuple-element.18), channel_id=1, source_target_pairs={{0,8},{8,0},{16,24},{24,16},{32,40},{40,32},{48,56},{56,48},{64,72... | collective-permute-start | bytes 995336 | tf_op jit(solution)/shard_map/ppermute | solution.py:414
  11.7 1.8 %collective-permute-done.got_ref = bf16[1296,128]{1,0:T(8,128)(2,1)S(1)} collective-permute-done((bf16[1296,128]{1,0:T(8,128)(2,1)}, bf16[1296,128]{1,0:T(8,128)(2,1)S(1)}, u32[]{:S(2)}, u32[]{:S(2)}) %collective-permute-start) | collective-permute-done | bytes 331808 | tf_op jit(solution)/shard_map/ppermute | solution.py:414
  13.5 1.0 copy-done
  14.5 1.8 %local.1 = (bf16[16,72,128]{2,1,0:T(8,128)(2,1)S(1)}, f32[2,4,128,128]{3,2,1,0:T(8,128)S(1)}, f32[128,16]{1,0:T(8,128)S(1)}) custom-call(bf16[1440,128]{1,0:T(8,128)(2,1)S(1)} %copy-done, bf16[1296,128]{1,0:T(8,128)(2,1)S(1)} %collective-permute-done.got_ref), custom_call_target="tpu_custom_call" | custom-call | flops 1000000000 | bytes 1000000 | tf_op jit(solution)/shard_map/local/pallas_call | solution.py:212
  16.2 0.0 copy-start.4
  16.3 50.6 %all_to_all.10.states_ref = bf16[16,72,128]{2,1,0:T(8,128)(2,1)S(1)} all-to-all(bf16[16,72,128]{2,1,0:T(8,128)(2,1)S(1)} %get-tuple-element.19), channel_id=1, replica_groups={{0,16,32,48,64,80,96,112,128,144,160,176,192,208,224,240},{8,24,40,56,7..., dimensions={0} | all-to-all | bytes 589824 | tf_op jit(solution)/shard_map/all_to_all | solution.py:448
  66.9 0.1 chain.1
  66.9 26.0 %all_to_all.11.entering_ref = bf16[16,64,128]{2,1,0:T(8,128)(2,1)S(1)} all-to-all(bf16[16,64,128]{2,1,0:T(8,128)(2,1)S(1)} %chain.1), channel_id=1, replica_groups={{0,16,32,48,64,80,96,112,128,144,160,176,192,208,224,240},{8,24,40,56,7..., dimensions={0} | all-to-all | bytes 524288 | tf_op jit(solution)/shard_map/all_to_all | solution.py:449
  92.9 0.4 gate.1
  93.3 0.0 copy-start.2
  93.4 0.7 collective-permute-start.3
  94.0 0.7 collective-permute-start.5
  94.7 2.0 %collective-permute-start.7 = (bf16[64,512]{1,0:T(8,128)(2,1)S(1)}, bf16[64,512]{1,0:T(8,128)(2,1)S(1)}, u32[]{:S(2)}, u32[]{:S(2)}) collective-permute-start(bf16[64,512]{1,0:T(8,128)(2,1)S(1)} %copy-done.4), channel_id=1, source_target_pairs={{0,0},{8,248},{16,8},{24,240},{32,16},{40,232},{48,24},{56,224},{6... | collective-permute-start | bytes 196616 | tf_op jit(solution)/shard_map/ppermute | solution.py:414
  96.7 11.4 %collective-permute-start.8 = (bf16[64,512]{1,0:T(8,128)(2,1)S(1)}, bf16[64,512]{1,0:T(8,128)(2,1)S(1)}, u32[]{:S(2)}, u32[]{:S(2)}) collective-permute-start(bf16[64,512]{1,0:T(8,128)(2,1)S(1)} %copy-done.3), channel_id=1, source_target_pairs={{0,248},{8,0},{16,240},{24,8},{32,232},{40,16},{48,224},{56,24},{6... | collective-permute-start | bytes 196616 | tf_op jit(solution)/shard_map/ppermute | solution.py:414
  108.1 2.0 %collective-permute-start.1 = (bf16[128,512]{1,0:T(8,128)(2,1)S(1)}, bf16[128,512]{1,0:T(8,128)(2,1)S(1)}, u32[]{:S(2)}, u32[]{:S(2)}) collective-permute-start(bf16[128,512]{1,0:T(8,128)(2,1)S(1)} %get-tuple-element.22), channel_id=1, source_target_pairs={{0,0},{8,248},{16,8},{24,240},{32,16},{40,232},{48,24},{56,224},{6... | collective-permute-start | bytes 393224 | tf_op jit(solution)/shard_map/ppermute | solution.py:414
  110.0 26.2 %collective-permute-done.7.q0_ref = bf16[64,512]{1,0:T(8,128)(2,1)S(1)} collective-permute-done((bf16[64,512]{1,0:T(8,128)(2,1)S(1)}, bf16[64,512]{1,0:T(8,128)(2,1)S(1)}, u32[]{:S(2)}, u32[]{:S(2)}) %collective-permute-start.7) | collective-permute-done | bytes 65568 | tf_op jit(solution)/shard_map/ppermute | solution.py:414
  136.2 1.9 %collective-permute-start.2 = (bf16[128,512]{1,0:T(8,128)(2,1)S(1)}, bf16[128,512]{1,0:T(8,128)(2,1)S(1)}, u32[]{:S(2)}, u32[]{:S(2)}) collective-permute-start(bf16[128,512]{1,0:T(8,128)(2,1)S(1)} %get-tuple-element.23), channel_id=1, source_target_pairs={{0,248},{8,0},{16,240},{24,8},{32,232},{40,16},{48,224},{56,24},{6... | collective-permute-start | bytes 393224 | tf_op jit(solution)/shard_map/ppermute | solution.py:414
  138.2 0.0 collective-permute-done.3
  138.2 0.7 collective-permute-start.4
  138.9 0.0 collective-permute-done.5
  138.9 0.7 collective-permute-start.6
  139.6 0.0 all-gather.3.cloned.1.call-done
  139.6 0.6 copy-done.6
  140.2 5.0 %attend.1 = bf16[128,512]{1,0:T(8,128)(2,1)} custom-call(bf16[64,512]{1,0:T(8,128)(2,1)} %copy-done.5, bf16[64,512]{1,0:T(8,128)(2,1)} %copy-done.6, bf16[32,256,128]{2,1,0:T(8,128)(2,1)} %bitcast.5), custom_call_target="tpu_custom_call" | custom-call | flops 1073741824 | bytes 1048576 | tf_op jit(solution)/shard_map/attend/pallas_call | solution.py:395
  145.2 0.0 collective-permute-done.1.even_ref
  145.2 2.2 %collective-permute-done.2.odd_ref = bf16[128,512]{1,0:T(8,128)(2,1)S(1)} collective-permute-done((bf16[128,512]{1,0:T(8,128)(2,1)S(1)}, bf16[128,512]{1,0:T(8,128)(2,1)S(1)}, u32[]{:S(2)}, u32[]{:S(2)}) %collective-permute-start.2) | collective-permute-done | bytes 131104 | tf_op jit(solution)/shard_map/ppermute | solution.py:414
  147.3 0.0 collective-permute-done.4.even_far_ref
  147.3 0.0 collective-permute-done.6.odd_far_ref
  147.3 0.9 norm.1
  (11 shorter events, 0.0 us)
Async XLA Ops:
  7.2 132.4 %all-gather.3.cloned.1.call-start = ((), (), s32[]{:S(2)}) async-start(), calls=%async_computation.2 | async-start | bytes 2162688 | tf_op jit(solution)/shard_map/all_gather | solution.py:437
  9.7 3.8 %collective-permute-start = (bf16[1296,128]{1,0:T(8,128)(2,1)}, bf16[1296,128]{1,0:T(8,128)(2,1)S(1)}, u32[]{:S(2)}, u32[]{:S(2)}) collective-permute-start(bf16[1296,128]{1,0:T(8,128)(2,1)} %get-tuple-element.18), channel_id=1, source_target_pairs={{0,8},{8,0},{16,24},{24,16},{32,40},{40,32},{48,56},{56,48},{64,72... | collective-permute-start | bytes 995336 | tf_op jit(solution)/shard_map/ppermute | solution.py:414
  13.5 1.0 copy-start
  14.5 78.4 %copy-start.1 = (bf16[1440,128]{1,0:T(8,128)(2,1)S(1)}, bf16[1440,128]{1,0:T(8,128)(2,1)}, u32[]{:S(2)}) copy-start(bf16[1440,128]{1,0:T(8,128)(2,1)} %get-tuple-element.17.mine_ref) | copy-start | bytes 1105924
  16.2 78.5 %copy-start.4 = (bf16[64,512]{1,0:T(8,128)(2,1)S(1)}, bf16[64,512]{1,0:T(8,128)(2,1)}, u32[]{:S(2)}) copy-start(bf16[64,512]{1,0:T(8,128)(2,1)} %get-tuple-element.24) | copy-start | bytes 196612
  16.2 80.4 %copy-start.3 = (bf16[64,512]{1,0:T(8,128)(2,1)S(1)}, bf16[64,512]{1,0:T(8,128)(2,1)}, u32[]{:S(2)}) copy-start(bf16[64,512]{1,0:T(8,128)(2,1)} %get-tuple-element.25) | copy-start | bytes 196612
  93.3 54.0 %copy-start.2 = (f32[1024]{0:T(1024)S(1)}, f32[1024]{0:T(1024)}, u32[]{:S(2)}) copy-start(f32[1024]{0:T(1024)} %param.23) | copy-start | bytes 12292
  93.4 44.8 %collective-permute-start.3 = (bf16[128,512]{1,0:T(8,128)(2,1)S(1)}, bf16[128,512]{1,0:T(8,128)(2,1)S(1)}, u32[]{:S(2)}, u32[]{:S(2)}) collective-permute-start(bf16[128,512]{1,0:T(8,128)(2,1)S(1)} %get-tuple-element.22), channel_id=1, source_target_pairs={{240,96},{248,104},{241,97},{249,105},{242,98},{250,106},{243,99},... | collective-permute-start | bytes 393224 | tf_op jit(solution)/shard_map/ppermute | solution.py:414
  94.0 44.8 %collective-permute-start.5 = (bf16[128,512]{1,0:T(8,128)(2,1)S(1)}, bf16[128,512]{1,0:T(8,128)(2,1)S(1)}, u32[]{:S(2)}, u32[]{:S(2)}) collective-permute-start(bf16[128,512]{1,0:T(8,128)(2,1)S(1)} %get-tuple-element.23), channel_id=1, source_target_pairs={{240,96},{248,104},{241,97},{249,105},{242,98},{250,106},{243,99},... | collective-permute-start | bytes 393224 | tf_op jit(solution)/shard_map/ppermute | solution.py:414
  94.7 41.5 %collective-permute-start.7 = (bf16[64,512]{1,0:T(8,128)(2,1)S(1)}, bf16[64,512]{1,0:T(8,128)(2,1)S(1)}, u32[]{:S(2)}, u32[]{:S(2)}) collective-permute-start(bf16[64,512]{1,0:T(8,128)(2,1)S(1)} %copy-done.4), channel_id=1, source_target_pairs={{0,0},{8,248},{16,8},{24,240},{32,16},{40,232},{48,24},{56,224},{6... | collective-permute-start | bytes 196616 | tf_op jit(solution)/shard_map/ppermute | solution.py:414
  96.7 42.8 %collective-permute-start.8 = (bf16[64,512]{1,0:T(8,128)(2,1)S(1)}, bf16[64,512]{1,0:T(8,128)(2,1)S(1)}, u32[]{:S(2)}, u32[]{:S(2)}) collective-permute-start(bf16[64,512]{1,0:T(8,128)(2,1)S(1)} %copy-done.3), channel_id=1, source_target_pairs={{0,248},{8,0},{16,240},{24,8},{32,232},{40,16},{48,224},{56,24},{6... | collective-permute-start | bytes 196616 | tf_op jit(solution)/shard_map/ppermute | solution.py:414
  108.1 37.1 %collective-permute-start.1 = (bf16[128,512]{1,0:T(8,128)(2,1)S(1)}, bf16[128,512]{1,0:T(8,128)(2,1)S(1)}, u32[]{:S(2)}, u32[]{:S(2)}) collective-permute-start(bf16[128,512]{1,0:T(8,128)(2,1)S(1)} %get-tuple-element.22), channel_id=1, source_target_pairs={{0,0},{8,248},{16,8},{24,240},{32,16},{40,232},{48,24},{56,224},{6... | collective-permute-start | bytes 393224 | tf_op jit(solution)/shard_map/ppermute | solution.py:414
  136.2 3.4 %copy-start.5 = (bf16[64,512]{1,0:T(8,128)(2,1)}, bf16[64,512]{1,0:T(8,128)(2,1)S(1)}, u32[]{:S(2)}) copy-start(bf16[64,512]{1,0:T(8,128)(2,1)S(1)} %collective-permute-done.7.q0_ref) | copy-start | bytes 196612
  136.2 11.1 %collective-permute-start.2 = (bf16[128,512]{1,0:T(8,128)(2,1)S(1)}, bf16[128,512]{1,0:T(8,128)(2,1)S(1)}, u32[]{:S(2)}, u32[]{:S(2)}) collective-permute-start(bf16[128,512]{1,0:T(8,128)(2,1)S(1)} %get-tuple-element.23), channel_id=1, source_target_pairs={{0,248},{8,0},{16,240},{24,8},{32,232},{40,16},{48,224},{56,24},{6... | collective-permute-start | bytes 393224 | tf_op jit(solution)/shard_map/ppermute | solution.py:414
  138.2 9.2 %collective-permute-start.4 = (bf16[128,512]{1,0:T(8,128)(2,1)S(1)}, bf16[128,512]{1,0:T(8,128)(2,1)S(1)}, u32[]{:S(2)}, u32[]{:S(2)}) collective-permute-start(bf16[128,512]{1,0:T(8,128)(2,1)S(1)} %collective-permute-done.3), channel_id=1, source_target_pairs={{96,120},{104,128},{97,121},{105,129},{98,122},{106,130},{99,123},... | collective-permute-start | bytes 393224 | tf_op jit(solution)/shard_map/ppermute | solution.py:428
  138.9 8.5 %collective-permute-start.6 = (bf16[128,512]{1,0:T(8,128)(2,1)S(1)}, bf16[128,512]{1,0:T(8,128)(2,1)S(1)}, u32[]{:S(2)}, u32[]{:S(2)}) collective-permute-start(bf16[128,512]{1,0:T(8,128)(2,1)S(1)} %collective-permute-done.5), channel_id=1, source_target_pairs={{96,128},{104,120},{97,129},{105,121},{98,130},{106,122},{99,131},... | collective-permute-start | bytes 393224 | tf_op jit(solution)/shard_map/ppermute | solution.py:428
  139.5 0.6 copy-start.6
Sparse Core Ops, SparseCore 0:
  10.7 98.6 all-gather.2
